TPU v7x, 32 devices: a whole 2x2x4 slice. The times are simulated.
32 devices in a mesh: row: 8 (over z, core), col: 4 (over y, x).
Axes of the slice: x: 2, y: 2, z: 4, core: 2. Of those that a mesh axis runs over, the one named last changes fastest.
Arguments:
- features: bfloat16 [8, 4, 1024, 602], P('row', 'col'), may hold values from -6 to 6
- local_mask: int32 [8, 4, 1024, 1024], P('row', 'col'), may hold values 0 or 1
- halo_mask: int32 [8, 4, 1024, 512], P('row', 'col'), may hold values 0 or 1
- boundary_index: int32 [8, 4, 512], P('row', 'col'), may hold values from 0 to 1023
- labels: int32 [8, 4, 1024], P('row', 'col'), may hold values from 0 to 40
- halo_first: bfloat16 [8, 4, 512, 602], P('row', 'col'), may hold values from -6 to 6
- halo_second: bfloat16 [8, 4, 512, 256], P('row', 'col'), may hold values from -4 to 4
- halo_third: bfloat16 [8, 4, 512, 256], P('row', 'col'), may hold values from -4 to 4
- return_second: bfloat16 [8, 4, 512, 256], P('row', 'col'), may hold values from -0.0059814453 to 0.0059814453
- return_third: bfloat16 [8, 4, 512, 256], P('row', 'col'), may hold values from -0.0059814453 to 0.0059814453
- weight_first: bfloat16 [602, 256], replicated, may hold values from -1 to 1
- weight_second: bfloat16 [256, 256], replicated, may hold values from -1.5 to 1.5
- weight_third: bfloat16 [256, 41], replicated, may hold values from -1.5 to 1.5
Outputs:
- grad_first: float32 [602, 256], replicated
- grad_second: float32 [256, 256], replicated
- grad_third: float32 [256, 41], replicated
- next_second: bfloat16 [8, 4, 512, 256], P('row', 'col')
- next_third: bfloat16 [8, 4, 512, 256], P('row', 'col')
- back_second: bfloat16 [8, 4, 512, 256], P('row', 'col')
- back_third: bfloat16 [8, 4, 512, 256], P('row', 'col')
All inputs are finite; a program needn't handle non-finite values. No bound on the sum of `local_mask` or of `halo_mask` on one device may be relied on, other than what follows from the above.
Results may differ from a plain program's by a relative error of at most 0.007.
Values may be sent and summed in bfloat16 or wider, within the bound.
A program may use at most 64 MiB of HBM per device.

v0:
```python
import functools

import jax
import jax.numpy as jnp
from jax import lax
from jax.experimental import pallas as pl
from jax.experimental.pallas import tpu as pltpu
from jax.sharding import PartitionSpec as P

MESH = pl.DeviceIdType.MESH
BF = jnp.bfloat16
F32 = jnp.float32


def up_to(value, step):
    return -(-value // step) * step


def dot(a, b, dims=((1,), (0,))):
    return lax.dot_general(a, b, (dims, ((), ())), preferred_element_type=F32)


def slope(pre):
    sigma = jax.nn.sigmoid(pre)
    return sigma * (1.0 + pre * (1.0 - sigma))


class Plan:
    def __init__(self, mesh, first, second, third):
        self.n_row, self.n_col = mesh.shape["row"], mesh.shape["col"]
        self.pair = 2 if self.n_row % 2 == 0 else 1
        self.deep = self.n_row // self.pair
        self.small = 16
        self.quarter = self.small * self.deep
        self.half = self.quarter * self.n_col
        self.piece = self.half * self.pair
        self.lanes = 128 if first[1] % 128 == 0 else first[1]
        self.strips = first[1] // self.lanes
        self.at_second = 0
        self.early = up_to(up_to(second[0], 16) * self.strips, self.piece) // self.piece
        self.at_first = self.early * self.piece
        self.at_third = self.at_first + up_to(first[0], 16) * self.strips
        self.pieces = up_to(self.at_third + up_to(third[0], 16) * self.strips, self.piece) // self.piece
        self.total = self.pieces * self.piece

    def strip(self, at, count, j):
        at = at + j * up_to(count, 16)
        return slice(at, at + count), slice(j * self.lanes, (j + 1) * self.lanes)

    def place(self):
        self.r, self.c = lax.axis_index("row"), lax.axis_index("col")
        self.core, self.z = self.r % self.pair, self.r // self.pair
        self.mate = self.r + 1 - 2 * self.core

    def col_peer(self, d):
        return (self.c + d) % self.n_col

    def deep_peer(self, d):
        return (self.z + d) % self.deep

    def deep_id(self, d):
        return (self.deep_peer(d) * self.pair + self.core, self.c)

    def greet(self):
        barrier = pltpu.get_barrier_semaphore()

        def hello(device):
            pl.semaphore_signal(barrier, inc=1, device_id=device, device_id_type=MESH)

        count = 0
        if self.pair == 2:
            hello((self.mate, self.c))
            count += 1
        for d in range(1, self.n_col):
            hello((self.r, self.col_peer(d)))
            count += 1
        for d in range(1, self.deep):
            hello(self.deep_id(d))
            count += 1
        for step, there in self.far_rows():
            @pl.when(there)
            def _():
                hello((self.r + step, self.c))
        for _, there in self.far_rows():
            count = count + jnp.where(there, 1, 0)
        pl.semaphore_wait(barrier, count)

    def far_rows(self):
        if self.pair == 2:
            return ((-1, jnp.logical_and(self.core == 0, self.r > 0)),
                    (1, jnp.logical_and(self.core == 1, self.r < self.n_row - 1)))
        return ()

    def edges(self):
        r, c = self.r, self.c
        return (((r - 1, c), 1, r > 0), ((r + 1, c), 0, r < self.n_row - 1),
                ((r, c - 1), 3, c > 0), ((r, c + 1), 2, c < self.n_col - 1))


def rows_at(start, count):
    return pl.ds(pl.multiple_of(start, 16), count)


def halo_copy(plan, k, src, dst, send, recv, way):
    bound = src.shape[0] // 4
    device, slot, there = plan.edges()[k]
    copy = pltpu.make_async_remote_copy(
        src_ref=src.at[pl.ds(k * bound, bound)], dst_ref=dst.at[pl.ds(slot * bound, bound)],
        send_sem=send.at[way, k], recv_sem=recv.at[way, slot], device_id=device, device_id_type=MESH)
    return copy, slot, there


def halo_start(plan, src, dst, send, recv, way):
    bound = src.shape[0] // 4
    for k in range(4):
        copy, _, there = halo_copy(plan, k, src, dst, send, recv, way)

        @pl.when(there)
        def _():
            copy.start()

        @pl.when(jnp.logical_not(there))
        def _():
            dst[pl.ds(k * bound, bound), :] = jnp.zeros((bound, dst.shape[1]), dst.dtype)


def halo_finish(plan, src, dst, send, recv, way):
    bound = src.shape[0] // 4
    for k in range(4):
        copy, _, there = halo_copy(plan, k, src, dst, send, recv, way)
        arrival = pltpu.make_async_remote_copy(
            src_ref=src.at[pl.ds(k * bound, bound)], dst_ref=dst.at[pl.ds(k * bound, bound)],
            send_sem=send.at[way, k], recv_sem=recv.at[way, k], device_id=plan.edges()[k][0], device_id_type=MESH)

        @pl.when(there)
        def _():
            copy.wait_send()
            arrival.wait_recv()


class Summer:
    STAGES = 6

    def __init__(self, plan, packed, packed_bf, got_pair, got_col, got_deep, acc_bf, whole, sems):
        self.plan, self.packed, self.packed_bf, self.whole = plan, packed, packed_bf, whole
        self.got_pair, self.got_col, self.got_deep, self.acc_bf = got_pair, got_col, got_deep, acc_bf
        self.sems = sems
        self.flying = {}
        self.stage = [0] * plan.pieces

    def copy(self, p, src, dst, kind, d, device):
        copy = pltpu.make_async_remote_copy(
            src_ref=src, dst_ref=dst, send_sem=self.sems[2 * kind].at[p, d], recv_sem=self.sems[2 * kind + 1].at[p, d],
            device_id=device, device_id_type=MESH)
        copy.start()
        self.flying[p].append(copy)

    def land(self, p):
        for copy in self.flying.get(p, ()):
            copy.wait()
        self.flying[p] = []

    def advance(self, p):
        plan, base = self.plan, p * self.plan.piece
        half, quarter, small = plan.half, plan.quarter, plan.small
        mine = base + plan.core * half
        own = mine + plan.c * quarter
        last = own + plan.z * small
        packed, whole, acc = self.packed, self.whole, self.acc_bf.at[p]
        stage = self.stage[p]
        self.stage[p] += 1
        self.land(p)
        if stage == 0 and plan.pair == 2:
            self.copy(p, self.packed_bf.at[rows_at(base + (1 - plan.core) * half, half)], self.got_pair.at[p], 0, 0, (plan.mate, plan.c))
        elif stage == 1:
            total = packed[rows_at(mine, half), :]
            if plan.pair == 2:
                total = total + self.got_pair[p].astype(F32)
            packed[rows_at(mine, half), :] = total
            acc[...] = total.astype(BF)
            for d in range(1, plan.n_col):
                peer = plan.col_peer(d)
                self.copy(p, acc.at[rows_at(peer * quarter, quarter)], self.got_col.at[p, d - 1], 1, d - 1, (plan.r, peer))
        elif stage == 2:
            total = packed[rows_at(own, quarter), :]
            for d in range(1, plan.n_col):
                total = total + self.got_col[p, d - 1].astype(F32)
            packed[rows_at(own, quarter), :] = total
            acc[0:quarter, :] = total.astype(BF)
            for d in range(1, plan.deep):
                self.copy(p, acc.at[rows_at(plan.deep_peer(d) * small, small)], self.got_deep.at[p, d - 1], 2, d - 1, plan.deep_id(d))
        elif stage == 3:
            total = packed[rows_at(last, small), :]
            for d in range(1, plan.deep):
                total = total + self.got_deep[p, d - 1].astype(F32)
            whole[rows_at(last, small), :] = total.astype(BF)
            part = whole.at[rows_at(last, small)]
            for d in range(1, plan.deep):
                self.copy(p, part, part, 3, d - 1, plan.deep_id(d))
        elif stage == 4:
            part = whole.at[rows_at(own, quarter)]
            for d in range(1, plan.n_col):
                self.copy(p, part, part, 4, d - 1, (plan.r, plan.col_peer(d)))
        elif stage == 5 and plan.pair == 2:
            part = whole.at[rows_at(mine, half)]
            self.copy(p, part, part, 5, 0, (plan.mate, plan.c))


NAMES = ("local", "halo", "features", "halo_first", "halo_second", "halo_third", "return_second", "return_third",
         "weight_first", "weight_second", "weight_third", "index_row", "labels")


def step_kernel(plan, tiles, *refs):
    count = len(NAMES)
    hbm = dict(zip(NAMES, refs[:count]))
    whole, n2, n3, b2, b3 = refs[count:count + 5]
    held = dict(zip(NAMES, refs[count + 5:2 * count + 5]))
    (in_sem, local_bf, halo_bf, inverse, hits, hits_t, mixed_one, mixed_two, mixed_three, pre_one, pre_two, hidden_one,
     hidden_two, scaled, upstream, upstream_three, target_held, s2, s3, o2, o3, hsend, hrecv,
     packed, packed_bf, got_pair, got_col, got_deep, acc_bf) = refs[2 * count + 5:2 * count + 34]
    sems = refs[2 * count + 34:]
    nodes = held["local"].shape[0]
    tall = nodes // tiles
    tile = [pl.ds(t * tall, tall) for t in range(tiles)]
    plan.place()

    loads = {}
    for name in ("index_row", "features", "halo_first", "local", "halo") + NAMES[4:11] + ("labels",):
        if name in ("local", "halo"):
            for t in range(tiles):
                key = (name, t)
                loads[key] = pltpu.make_async_copy(hbm[name].at[tile[t]], held[name].at[tile[t]], in_sem.at[len(loads)])
        else:
            loads[name] = pltpu.make_async_copy(hbm[name], held[name], in_sem.at[len(loads)])
    order = ["index_row", "features", "halo_first"]
    for t in range(tiles):
        order += [("local", t), ("halo", t)]
    order += [name for name in loads if name not in order]
    for key in order:
        loads[key].start()

    plan.greet()
    packed[...] = jnp.zeros_like(packed)
    packed_bf[...] = jnp.zeros_like(packed_bf)
    summer = Summer(plan, packed, packed_bf, got_pair, got_col, got_deep, acc_bf, whole, sems)

    def put(value, at):
        for j in range(plan.strips):
            rows, lanes = plan.strip(at, value.shape[0], j)
            packed[rows, :] = value[:, lanes]
            packed_bf[rows, :] = value[:, lanes].astype(BF)

    loads["index_row"].wait()
    slots = hits.shape[1]
    hits[...] = jnp.where(lax.broadcasted_iota(jnp.int32, (nodes, slots), 0) == held["index_row"][...], 1.0, 0.0).astype(BF)
    hits_t[...] = hits[...].T
    loads["labels"].wait()
    wide = target_held.shape[1]
    target_held[...] = jnp.where(lax.broadcasted_iota(jnp.int32, (wide, nodes), 0) == held["labels"][...], 1.0, 0.0).T
    loads["features"].wait()
    loads["halo_first"].wait()

    def spread(t, values, remote, out, dims=((1,), (0,))):
        total = dot(local_bf[tile[t], :], values[...], dims) + dot(halo_bf[tile[t], :], remote[...], dims)
        out[tile[t], :] = (total * inverse[tile[t], :]).astype(BF)

    for t in range(tiles):
        loads[("local", t)].wait()
        loads[("halo", t)].wait()
        near, far = held["local"][tile[t], :].astype(F32), held["halo"][tile[t], :].astype(F32)
        here = lax.broadcasted_iota(jnp.int32, near.shape, 0) + t * tall == lax.broadcasted_iota(jnp.int32, near.shape, 1)
        local_bf[tile[t], :] = jnp.where(here, near + 1.0, near).astype(BF)
        halo_bf[tile[t], :] = far.astype(BF)
        inverse[tile[t], :] = 1.0 / (1.0 + jnp.sum(near, axis=1, keepdims=True) + jnp.sum(far, axis=1, keepdims=True))
        spread(t, held["features"], held["halo_first"], mixed_one, ((1,), (1,)))
        if t == 0:
            for name in NAMES[4:11]:
                loads[name].wait()
        pre = dot(mixed_one[tile[t], :], held["weight_first"][...])
        pre_one[tile[t], :] = pre
        hidden_one[tile[t], :] = (pre * jax.nn.sigmoid(pre)).astype(BF)
    s2[...] = dot(hits_t[...], hidden_one[...]).astype(BF)
    halo_start(plan, s2, n2, hsend, hrecv, 0)
    for t in range(tiles):
        spread(t, hidden_one, held["halo_second"], mixed_two)
        pre = dot(mixed_two[tile[t], :], held["weight_second"][...])
        pre_two[tile[t], :] = pre
        hidden_two[tile[t], :] = (pre * jax.nn.sigmoid(pre)).astype(BF)
    s3[...] = dot(hits_t[...], hidden_two[...]).astype(BF)
    halo_start(plan, s3, n3, hsend, hrecv, 1)
    for t in range(tiles):
        spread(t, hidden_two, held["halo_third"], mixed_three)
        logits = dot(mixed_three[tile[t], :], held["weight_third"][...], ((1,), (1,)))
        expo = jnp.exp(logits)
        probs = expo / jnp.sum(expo, axis=1, keepdims=True)
        target = target_held[tile[t], :logits.shape[1]]
        up = ((probs - target) / nodes).astype(BF)
        upstream_three[tile[t], :] = up
        scaled[tile[t], :] = (dot(up, held["weight_third"][...]) * inverse[tile[t], :]).astype(BF)
    turn = ((0,), (0,))

    def carry(t, returned):
        return dot(local_bf[:, tile[t]], scaled[...], turn) + dot(hits[tile[t], :], returned[...])

    for t in range(tiles):
        upstream[tile[t], :] = (carry(t, held["return_third"]) * slope(pre_two[tile[t], :])).astype(BF)
    put(dot(mixed_two[...], upstream[...], turn), plan.at_second)
    for p in range(plan.early):
        summer.advance(p)
    o3[...] = dot(halo_bf[...], scaled[...], turn).astype(BF)
    halo_start(plan, o3, b3, hsend, hrecv, 2)
    put(dot(upstream_three[...], mixed_three[...], turn), plan.at_third)
    for t in range(tiles):
        across = dot(upstream[tile[t], :], held["weight_second"][...], ((1,), (1,)))
        scaled[tile[t], :] = (across * inverse[tile[t], :]).astype(BF)
    for p in range(plan.early):
        summer.advance(p)
    for t in range(tiles):
        upstream[tile[t], :] = (carry(t, held["return_second"]) * slope(pre_one[tile[t], :])).astype(BF)
    for p in range(plan.early):
        summer.advance(p)
    put(dot(mixed_one[...], upstream[...], turn), plan.at_first)
    for p in range(plan.early, plan.pieces):
        summer.advance(p)
    for p in range(plan.early):
        summer.advance(p)
    o2[...] = dot(halo_bf[...], scaled[...], turn).astype(BF)
    halo_start(plan, o2, b2, hsend, hrecv, 3)
    for stage in range(1, Summer.STAGES):
        for p in list(range(plan.early, plan.pieces)) + list(range(plan.early)):
            if summer.stage[p] < Summer.STAGES:
                summer.advance(p)
    for p in range(plan.pieces):
        summer.land(p)
    for way, (src, dst) in enumerate(((s2, n2), (s3, n3), (o3, b3), (o2, b2))):
        halo_finish(plan, src, dst, hsend, hrecv, way)


def finish_kernel(plan, whole, n2, n3, b2, b3, g1, g2, g3, m2, m3, a2, a3, h1, h2, h3, sem):
    copies = [pltpu.make_async_copy(src, dst, sem.at[i]) for i, (src, dst) in enumerate(((n2, m2), (n3, m3), (b2, a2), (b3, a3)))]
    for copy in copies:
        copy.start()
    for ref, at in ((h1, plan.at_first), (h2, plan.at_second), (h3, plan.at_third)):
        for j in range(plan.strips):
            rows, lanes = plan.strip(at, ref.shape[0], j)
            ref[:, lanes] = whole[rows, :].astype(F32)
    for i, (src, dst) in enumerate(((h1, g1), (h2, g2), (h3, g3))):
        copies.append(pltpu.make_async_copy(src, dst, sem.at[4 + i]))
        copies[-1].start()
    for copy in copies:
        copy.wait()


def per_device(mesh, features, local_mask, halo_mask, boundary_index, labels, halo_first, halo_second, halo_third,
               return_second, return_third, weight_first, weight_second, weight_third):
    features, local_mask, halo_mask = features[0, 0], local_mask[0, 0], halo_mask[0, 0]
    index, labels = boundary_index[0, 0], labels[0, 0]
    halo_first, halo_second, halo_third = halo_first[0, 0], halo_second[0, 0], halo_third[0, 0]
    return_second, return_third = return_second[0, 0], return_third[0, 0]
    nodes, width = features.shape
    slots, hidden, classes = index.shape[0], weight_first.shape[1], weight_third.shape[1]
    plan = Plan(mesh, weight_first.shape, weight_second.shape, weight_third.shape[::-1])
    tiles = 4 if nodes % 512 == 0 else 1
    values = (local_mask, halo_mask, features.T, halo_first.T, halo_second, halo_third, return_second, return_third,
              weight_first, weight_second, weight_third.T, index[None, :], labels[None, :])
    vmem, anywhere = pl.BlockSpec(memory_space=pltpu.VMEM), pl.BlockSpec(memory_space=pl.ANY)
    dma = pltpu.SemaphoreType.DMA
    peers, deep, n, lanes = max(plan.n_col - 1, 1), max(plan.deep - 1, 1), plan.pieces, plan.lanes
    block = jax.ShapeDtypeStruct((slots, hidden), BF)
    done = pl.pallas_call(
        functools.partial(step_kernel, plan, tiles),
        out_shape=(jax.ShapeDtypeStruct((plan.total, lanes), BF),) + (block,) * 4,
        in_specs=[anywhere] * len(values), out_specs=(vmem,) * 5,
        scratch_shapes=[pltpu.VMEM(v.shape, v.dtype) for v in values] + [
            dma((len(values) + 2 * tiles,)), pltpu.VMEM((nodes, nodes), BF), pltpu.VMEM((nodes, slots), BF), pltpu.VMEM((nodes, 1), F32),
            pltpu.VMEM((nodes, slots), BF), pltpu.VMEM((slots, nodes), BF),
            pltpu.VMEM((nodes, width), BF), pltpu.VMEM((nodes, hidden), BF), pltpu.VMEM((nodes, hidden), BF),
            pltpu.VMEM((nodes, hidden), F32), pltpu.VMEM((nodes, hidden), F32),
            pltpu.VMEM((nodes, hidden), BF), pltpu.VMEM((nodes, hidden), BF), pltpu.VMEM((nodes, hidden), BF),
            pltpu.VMEM((nodes, hidden), BF), pltpu.VMEM((nodes, classes), BF),
            pltpu.VMEM((nodes, up_to(classes, 128)), F32)]
        + [pltpu.VMEM((slots, hidden), BF)] * 4 + [dma((4, 4)), dma((4, 4)),
            pltpu.VMEM((plan.total, lanes), F32), pltpu.VMEM((plan.total, lanes), BF),
            pltpu.VMEM((n, plan.half, lanes), BF), pltpu.VMEM((n, peers, plan.quarter, lanes), BF),
            pltpu.VMEM((n, deep, plan.small, lanes), BF), pltpu.VMEM((n, plan.half, lanes), BF),
            dma((n, 1)), dma((n, 1)), dma((n, peers)), dma((n, peers)), dma((n, deep)), dma((n, deep)),
            dma((n, deep)), dma((n, deep)), dma((n, peers)), dma((n, peers)), dma((n, 1)), dma((n, 1))],
        compiler_params=pltpu.CompilerParams(collective_id=0, has_side_effects=True),
        name="step",
    )(*values)
    whole, n2, n3, b2, b3 = done
    grads = ((weight_first.shape, F32), (weight_second.shape, F32), (weight_third.shape[::-1], F32))
    out = pl.pallas_call(
        functools.partial(finish_kernel, plan),
        out_shape=tuple(jax.ShapeDtypeStruct(*g) for g in grads) + (block,) * 4,
        in_specs=[vmem] * 5, out_specs=(anywhere,) * 7,
        scratch_shapes=[pltpu.VMEM(*g) for g in grads] + [dma((7,))],
        name="finish",
    )(whole, n2, n3, b2, b3)
    return (out[0], out[1], out[2].T) + tuple(v[None, None] for v in out[3:])


def solution(mesh):
    wide, flat, copied = P("row", "col", None, None), P("row", "col", None), P()
    return jax.shard_map(
        functools.partial(per_device, mesh), mesh=mesh,
        in_specs=(wide, wide, wide, flat, flat, wide, wide, wide, wide, wide, copied, copied, copied),
        out_specs=(copied, copied, copied, wide, wide, wide, wide),
        check_vma=False,
    )
```

profile of v0, /device:TPU:0, one launch (start us, length us, event | category | flops | bytes accessed | tf_op | source)
XLA Modules:
  0.0 53.3 jit_solution(2743639316814240168)
XLA Ops:
  0.6 49.9 %step.1 = (bf16[2048,128]{1,0:T(8,128)(2,1)}, bf16[512,256]{1,0:T(8,128)(2,1)}, bf16[512,256]{1,0:T(8,128)(2,1)}, bf16[512,256]{1,0:T(8,128)(2,1)}, bf16[512,256]{1,0:T(8,128)(2,1)}) custom-call(s32[1024,1024]{1,0:T(8,128)} %bitcast.20, s32[1024,512]{1,0:T(8,128)} %bitcast.21, bf16[602,1024]{1,0:T(8,128)(2,1)} %bitcast.22, bf16[602,512]{1,0:T(8,128)(2,1)} %bitcast.23, ...), custom_call_target="tpu_custom_call" | custom-call | tf_op jit(solution)/shard_map/step/pallas_call | solution.py:370
  50.5 2.7 %finish.1 = (f32[602,256]{1,0:T(8,128)}, f32[256,256]{1,0:T(8,128)}, f32[41,256]{1,0:T(8,128)}, bf16[512,256]{1,0:T(8,128)(2,1)}, bf16[512,256]{1,0:T(8,128)(2,1...) custom-call(bf16[2048,128]{1,0:T(8,128)(2,1)} %get-tuple-element.19.whole, bf16[512,256]{1,0:T(8,128)(2,1)} %get-tuple-element.20.n2, ...), custom_call_target="tpu_custom_call" | custom-call | tf_op jit(solution)/shard_map/finish/pallas_call | solution.py:393
where the time goes:
time: 53.5 us; the launch traced here: 53.3 us
  Pallas kernels  52.5 us (98%)
  between operations  0.81 us (2%)
    pallas_call x1, Pallas kernels, per_device(): pl.pallas_call(functools.partial(step_kernel, plan, tiles), out_shape=(ja...  49.9 us
    pallas_call x1, Pallas kernels, per_device(): pl.pallas_call(functools.partial(finish_kernel, plan), out_shape=tuple((j...  2.66 us

commit v1 on v0

v1 whole, which is shorter than its diff:
```python
import functools

import jax
import jax.numpy as jnp
from jax import lax
from jax.experimental import pallas as pl
from jax.experimental.pallas import tpu as pltpu
from jax.sharding import PartitionSpec as P

MESH = pl.DeviceIdType.MESH
BF = jnp.bfloat16
F32 = jnp.float32


def up_to(value, step):
    return -(-value // step) * step


def dot(a, b, dims=((1,), (0,))):
    return lax.dot_general(a, b, (dims, ((), ())), preferred_element_type=F32)


def slope(pre):
    sigma = jax.nn.sigmoid(pre)
    return sigma * (1.0 + pre * (1.0 - sigma))


class Plan:
    def __init__(self, mesh, hidden):
        self.n_row, self.n_col = mesh.shape["row"], mesh.shape["col"]
        self.pair = 2 if self.n_row % 2 == 0 else 1
        self.deep = self.n_row // self.pair
        self.chips = self.deep * self.n_col
        self.lanes = hidden // self.pair
        deep = sorted(range(self.deep), key=lambda d: -min(d, self.deep - d))
        cols = sorted(range(self.n_col), key=lambda d: -min(d, self.n_col - d))
        self.ways = [(dz, dc) for dz in deep for dc in cols if dz or dc]

    def place(self):
        self.r, self.c = lax.axis_index("row"), lax.axis_index("col")
        self.core, self.z = self.r % self.pair, self.r // self.pair
        self.mate = self.r + 1 - 2 * self.core
        self.chip = self.z * self.n_col + self.c

    def peer(self, way, sign=1):
        z = (self.z + sign * way[0] + self.deep) % self.deep
        c = (self.c + sign * way[1] + self.n_col) % self.n_col
        return z * self.n_col + c, (z * self.pair + self.core, c)

    def greet(self):
        barrier = pltpu.get_barrier_semaphore()

        def hello(device):
            pl.semaphore_signal(barrier, inc=1, device_id=device, device_id_type=MESH)

        count = 0
        if self.pair == 2:
            hello((self.mate, self.c))
            count += 1
        for way in self.ways:
            hello(self.peer(way)[1])
            count += 1
        for step, there in self.far_rows():
            @pl.when(there)
            def _():
                hello((self.r + step, self.c))
        for _, there in self.far_rows():
            count = count + jnp.where(there, 1, 0)
        pl.semaphore_wait(barrier, count)

    def far_rows(self):
        if self.pair == 2:
            return ((-1, jnp.logical_and(self.core == 0, self.r > 0)),
                    (1, jnp.logical_and(self.core == 1, self.r < self.n_row - 1)))
        return ()

    def edges(self):
        r, c = self.r, self.c
        return (((r - 1, c), 1, r > 0), ((r + 1, c), 0, r < self.n_row - 1),
                ((r, c - 1), 3, c > 0), ((r, c + 1), 2, c < self.n_col - 1))


def halo_copy(plan, k, src, dst, send, recv, way):
    bound = src.shape[0] // 4
    device, slot, there = plan.edges()[k]
    copy = pltpu.make_async_remote_copy(
        src_ref=src.at[pl.ds(k * bound, bound)], dst_ref=dst.at[pl.ds(slot * bound, bound)],
        send_sem=send.at[way, k], recv_sem=recv.at[way, slot], device_id=device, device_id_type=MESH)
    return copy, slot, there


def halo_start(plan, src, dst, send, recv, way):
    bound = src.shape[0] // 4
    for k in range(4):
        copy, _, there = halo_copy(plan, k, src, dst, send, recv, way)

        @pl.when(there)
        def _():
            copy.start()

        @pl.when(jnp.logical_not(there))
        def _():
            dst[pl.ds(k * bound, bound), :] = jnp.zeros((bound, dst.shape[1]), dst.dtype)


def halo_finish(plan, src, dst, send, recv, way):
    bound = src.shape[0] // 4
    for k in range(4):
        copy, _, there = halo_copy(plan, k, src, dst, send, recv, way)
        arrival = pltpu.make_async_remote_copy(
            src_ref=src.at[pl.ds(k * bound, bound)], dst_ref=dst.at[pl.ds(k * bound, bound)],
            send_sem=send.at[way, k], recv_sem=recv.at[way, k], device_id=plan.edges()[k][0], device_id_type=MESH)

        @pl.when(there)
        def _():
            copy.wait_send()
            arrival.wait_recv()


class Summer:
    def __init__(self, plan, sizes, own, mine, got_pair, acc, got, whole, sems):
        self.plan, self.sizes, self.own, self.mine, self.got_pair = plan, sizes, own, mine, got_pair
        self.acc, self.got, self.whole, self.sems = acc, got, whole, sems

    def copy(self, src, dst, kind, d, device):
        return pltpu.make_async_remote_copy(
            src_ref=src, dst_ref=dst, send_sem=self.sems[2 * kind].at[d], recv_sem=self.sems[2 * kind + 1].at[d],
            device_id=device, device_id_type=MESH)

    def clear(self):
        self.own[...] = jnp.zeros_like(self.own)
        self.mine[...] = jnp.zeros_like(self.mine)

    def put(self, i, value):
        at, chunk = slabs(self.sizes, self.plan.chips)[i]
        for core in range(self.plan.pair):
            part = value[:, core * self.plan.lanes:(core + 1) * self.plan.lanes]
            for k in range(-(-value.shape[0] // chunk)):
                rows = part[k * chunk:(k + 1) * chunk]
                self.own[core, k, at:at + rows.shape[0], :] = rows
                self.mine[core, k, at:at + rows.shape[0], :] = rows.astype(BF)

    def pair_copy(self):
        return self.copy(self.mine.at[1 - self.plan.core], self.got_pair, 0, 0, (self.plan.mate, self.plan.c))

    def start_pair(self):
        if self.plan.pair == 2:
            self.pair_copy().start()

    def spread_copy(self, d):
        index, device = self.plan.peer(self.plan.ways[d])
        return self.copy(self.acc.at[index], self.got.at[d], 1, d, device)

    def start_spread(self):
        if self.plan.pair == 2:
            self.pair_copy().wait()
            self.acc[...] = (self.own[self.plan.core] + self.got_pair[...].astype(F32)).astype(BF)
        else:
            self.acc[...] = self.mine[0]
        for d in range(len(self.plan.ways)):
            self.spread_copy(d).start()

    def gather_copy(self, d):
        part = self.whole.at[self.plan.core, self.plan.chip]
        return self.copy(part, part, 2, d, self.plan.peer(self.plan.ways[d])[1])

    def back_copy(self, d, core):
        index = self.plan.chip if d == len(self.plan.ways) else self.plan.peer(self.plan.ways[d], -1)[0]
        part = self.whole.at[core, index]
        return self.copy(part, part, 3, d, (self.plan.mate, self.plan.c))

    def start_gather(self):
        plan = self.plan
        total = self.own[plan.core, plan.chip]
        if plan.pair == 2:
            total = total + self.got_pair[plan.chip].astype(F32)
        for d in range(len(plan.ways)):
            self.spread_copy(d).wait()
        for d in range(len(plan.ways)):
            total = total + self.got[d].astype(F32)
        self.whole[plan.core, plan.chip] = total.astype(BF)
        for d in range(len(plan.ways)):
            self.gather_copy(d).start()
        if plan.pair == 2:
            self.back_copy(len(plan.ways), plan.core).start()

    def start_back(self):
        plan = self.plan
        for d in reversed(range(len(plan.ways))):
            index = plan.peer(plan.ways[d], -1)[0]
            part = self.whole.at[plan.core, index]
            self.copy(part, part, 2, d, plan.peer(plan.ways[d], -1)[1]).wait_recv()
            if plan.pair == 2:
                self.back_copy(d, plan.core).start()

    def finish(self):
        plan = self.plan
        for d in range(len(plan.ways)):
            self.gather_copy(d).wait_send()
        if plan.pair == 2:
            for d in range(len(plan.ways) + 1):
                self.back_copy(d, plan.core).wait_send()
                self.back_copy(d, 1 - plan.core).wait_recv()


def slabs(sizes, chips):
    out, at = [], 0
    for size in sizes:
        chunk = up_to(-(-size // chips), 8)
        out.append((at, chunk))
        at += chunk
    return out


def slab_rows(sizes, chips):
    return sum(chunk for _, chunk in slabs(sizes, chips))


def summer_scratch(plan, sizes):
    rows, dma, n = slab_rows(sizes, plan.chips), pltpu.SemaphoreType.DMA, max(len(plan.ways), 1)
    full = (plan.chips, rows, plan.lanes)
    return [pltpu.VMEM((plan.pair,) + full, F32), pltpu.VMEM((plan.pair,) + full, BF), pltpu.VMEM(full, BF),
            pltpu.VMEM(full, BF), pltpu.VMEM((n, rows, plan.lanes), BF),
            dma((1,)), dma((1,)), dma((n,)), dma((n,)), dma((n,)), dma((n,)), dma((n + 1,)), dma((n + 1,))]


SUMMER_REFS = 13


NAMES = ("local", "halo", "features", "halo_first", "halo_second", "halo_third", "return_second", "return_third",
         "weight_first", "weight_second", "weight_third", "index_row", "labels")


def step_kernel(plan, tiles, early_sizes, late_sizes, *refs):
    count = len(NAMES)
    hbm = dict(zip(NAMES, refs[:count]))
    whole_early, whole_late, n2, n3, b2, b3 = refs[count:count + 6]
    held = dict(zip(NAMES, refs[count + 6:2 * count + 6]))
    (in_sem, local_bf, halo_bf, inverse, hits, hits_t, mixed_one, mixed_two, mixed_three, pre_one, pre_two, hidden_one,
     hidden_two, scaled, upstream, upstream_three, target_held, s2, s3, o2, o3, hsend, hrecv) = refs[2 * count + 6:2 * count + 29]
    rest = refs[2 * count + 29:]
    early, late = (Summer(plan, sizes, *part[:5], whole, part[5:]) for sizes, part, whole in (
        (early_sizes, rest[:SUMMER_REFS], whole_early), (late_sizes, rest[SUMMER_REFS:], whole_late)))
    nodes = held["local"].shape[0]
    tall = nodes // tiles
    tile = [pl.ds(t * tall, tall) for t in range(tiles)]
    plan.place()

    loads = {}
    for name in ("index_row", "features", "halo_first", "local", "halo") + NAMES[4:11] + ("labels",):
        if name in ("local", "halo"):
            for t in range(tiles):
                key = (name, t)
                loads[key] = pltpu.make_async_copy(hbm[name].at[tile[t]], held[name].at[tile[t]], in_sem.at[len(loads)])
        else:
            loads[name] = pltpu.make_async_copy(hbm[name], held[name], in_sem.at[len(loads)])
    order = ["index_row", "features", "halo_first"]
    for t in range(tiles):
        order += [("local", t), ("halo", t)]
    order += [name for name in loads if name not in order]
    for key in order:
        loads[key].start()

    plan.greet()
    early.clear()
    late.clear()

    loads["index_row"].wait()
    slots = hits.shape[1]
    hits[...] = jnp.where(lax.broadcasted_iota(jnp.int32, (nodes, slots), 0) == held["index_row"][...], 1.0, 0.0).astype(BF)
    hits_t[...] = hits[...].T
    loads["labels"].wait()
    wide = target_held.shape[1]
    target_held[...] = jnp.where(lax.broadcasted_iota(jnp.int32, (wide, nodes), 0) == held["labels"][...], 1.0, 0.0).T
    loads["features"].wait()
    loads["halo_first"].wait()

    def spread(t, values, remote, out, dims=((1,), (0,))):
        total = dot(local_bf[tile[t], :], values[...], dims) + dot(halo_bf[tile[t], :], remote[...], dims)
        out[tile[t], :] = (total * inverse[tile[t], :]).astype(BF)

    for t in range(tiles):
        loads[("local", t)].wait()
        loads[("halo", t)].wait()
        near, far = held["local"][tile[t], :].astype(F32), held["halo"][tile[t], :].astype(F32)
        here = lax.broadcasted_iota(jnp.int32, near.shape, 0) + t * tall == lax.broadcasted_iota(jnp.int32, near.shape, 1)
        local_bf[tile[t], :] = jnp.where(here, near + 1.0, near).astype(BF)
        halo_bf[tile[t], :] = far.astype(BF)
        inverse[tile[t], :] = 1.0 / (1.0 + jnp.sum(near, axis=1, keepdims=True) + jnp.sum(far, axis=1, keepdims=True))
        spread(t, held["features"], held["halo_first"], mixed_one, ((1,), (1,)))
        if t == 0:
            for name in NAMES[4:11]:
                loads[name].wait()
        pre = dot(mixed_one[tile[t], :], held["weight_first"][...])
        pre_one[tile[t], :] = pre
        hidden_one[tile[t], :] = (pre * jax.nn.sigmoid(pre)).astype(BF)
    s2[...] = dot(hits_t[...], hidden_one[...]).astype(BF)
    halo_start(plan, s2, n2, hsend, hrecv, 0)
    for t in range(tiles):
        spread(t, hidden_one, held["halo_second"], mixed_two)
        pre = dot(mixed_two[tile[t], :], held["weight_second"][...])
        pre_two[tile[t], :] = pre
        hidden_two[tile[t], :] = (pre * jax.nn.sigmoid(pre)).astype(BF)
    s3[...] = dot(hits_t[...], hidden_two[...]).astype(BF)
    halo_start(plan, s3, n3, hsend, hrecv, 1)
    for t in range(tiles):
        spread(t, hidden_two, held["halo_third"], mixed_three)
        logits = dot(mixed_three[tile[t], :], held["weight_third"][...], ((1,), (1,)))
        expo = jnp.exp(logits)
        probs = expo / jnp.sum(expo, axis=1, keepdims=True)
        target = target_held[tile[t], :logits.shape[1]]
        up = ((probs - target) / nodes).astype(BF)
        upstream_three[tile[t], :] = up
        scaled[tile[t], :] = (dot(up, held["weight_third"][...]) * inverse[tile[t], :]).astype(BF)
    turn = ((0,), (0,))

    def carry(t, returned):
        return dot(local_bf[:, tile[t]], scaled[...], turn) + dot(hits[tile[t], :], returned[...])

    for t in range(tiles):
        upstream[tile[t], :] = (carry(t, held["return_third"]) * slope(pre_two[tile[t], :])).astype(BF)
    early.put(0, dot(mixed_two[...], upstream[...], turn))
    early.put(1, dot(upstream_three[...], mixed_three[...], turn))
    early.start_pair()
    o3[...] = dot(halo_bf[...], scaled[...], turn).astype(BF)
    halo_start(plan, o3, b3, hsend, hrecv, 2)
    for t in range(tiles):
        across = dot(upstream[tile[t], :], held["weight_second"][...], ((1,), (1,)))
        scaled[tile[t], :] = (across * inverse[tile[t], :]).astype(BF)
    early.start_spread()
    for t in range(tiles):
        upstream[tile[t], :] = (carry(t, held["return_second"]) * slope(pre_one[tile[t], :])).astype(BF)
    late.put(0, dot(mixed_one[...], upstream[...], turn))
    late.start_pair()
    o2[...] = dot(halo_bf[...], scaled[...], turn).astype(BF)
    late.start_spread()
    early.start_gather()
    halo_start(plan, o2, b2, hsend, hrecv, 3)
    late.start_gather()
    early.start_back()
    late.start_back()
    early.finish()
    late.finish()
    for way, (src, dst) in enumerate(((s2, n2), (s3, n3), (o3, b3), (o2, b2))):
        halo_finish(plan, src, dst, hsend, hrecv, way)


def finish_kernel(plan, early_sizes, late_sizes, whole_early, whole_late, n2, n3, b2, b3, g1, g2, g3, m2, m3, a2, a3, h1, h2, h3, sem):
    copies = [pltpu.make_async_copy(src, dst, sem.at[i]) for i, (src, dst) in enumerate(((n2, m2), (n3, m3), (b2, a2), (b3, a3)))]
    for copy in copies:
        copy.start()
    for i, (ref, out, whole, sizes, part) in enumerate((
            (h1, g1, whole_late, late_sizes, 0), (h2, g2, whole_early, early_sizes, 0), (h3, g3, whole_early, early_sizes, 1))):
        at, chunk = slabs(sizes, plan.chips)[part]
        for core in range(plan.pair):
            for k in range(-(-ref.shape[0] // chunk)):
                rows = min(chunk, ref.shape[0] - k * chunk)
                ref[k * chunk:k * chunk + rows, core * plan.lanes:(core + 1) * plan.lanes] = whole[core, k, at:at + rows, :].astype(F32)
        copies.append(pltpu.make_async_copy(ref, out, sem.at[4 + i]))
        copies[-1].start()
    for copy in copies:
        copy.wait()


def per_device(mesh, features, local_mask, halo_mask, boundary_index, labels, halo_first, halo_second, halo_third,
               return_second, return_third, weight_first, weight_second, weight_third):
    features, local_mask, halo_mask = features[0, 0], local_mask[0, 0], halo_mask[0, 0]
    index, labels = boundary_index[0, 0], labels[0, 0]
    halo_first, halo_second, halo_third = halo_first[0, 0], halo_second[0, 0], halo_third[0, 0]
    return_second, return_third = return_second[0, 0], return_third[0, 0]
    nodes, width = features.shape
    slots, hidden, classes = index.shape[0], weight_first.shape[1], weight_third.shape[1]
    plan = Plan(mesh, hidden)
    early_sizes, late_sizes = (weight_second.shape[0], classes), (width,)
    tiles = 4 if nodes % 512 == 0 else 1
    values = (local_mask, halo_mask, features.T, halo_first.T, halo_second, halo_third, return_second, return_third,
              weight_first, weight_second, weight_third.T, index[None, :], labels[None, :])
    vmem, anywhere = pl.BlockSpec(memory_space=pltpu.VMEM), pl.BlockSpec(memory_space=pl.ANY)
    dma = pltpu.SemaphoreType.DMA
    block = jax.ShapeDtypeStruct((slots, hidden), BF)
    done = pl.pallas_call(
        functools.partial(step_kernel, plan, tiles, early_sizes, late_sizes),
        out_shape=tuple(jax.ShapeDtypeStruct((plan.pair, plan.chips, slab_rows(sizes, plan.chips), plan.lanes), BF)
                        for sizes in (early_sizes, late_sizes)) + (block,) * 4,
        in_specs=[anywhere] * len(values), out_specs=(vmem,) * 6,
        scratch_shapes=[pltpu.VMEM(v.shape, v.dtype) for v in values] + [
            dma((len(values) + 2 * tiles,)), pltpu.VMEM((nodes, nodes), BF), pltpu.VMEM((nodes, slots), BF), pltpu.VMEM((nodes, 1), F32),
            pltpu.VMEM((nodes, slots), BF), pltpu.VMEM((slots, nodes), BF),
            pltpu.VMEM((nodes, width), BF), pltpu.VMEM((nodes, hidden), BF), pltpu.VMEM((nodes, hidden), BF),
            pltpu.VMEM((nodes, hidden), F32), pltpu.VMEM((nodes, hidden), F32),
            pltpu.VMEM((nodes, hidden), BF), pltpu.VMEM((nodes, hidden), BF), pltpu.VMEM((nodes, hidden), BF),
            pltpu.VMEM((nodes, hidden), BF), pltpu.VMEM((nodes, classes), BF),
            pltpu.VMEM((nodes, up_to(classes, 128)), F32)]
        + [pltpu.VMEM((slots, hidden), BF)] * 4 + [dma((4, 4)), dma((4, 4))]
        + summer_scratch(plan, early_sizes) + summer_scratch(plan, late_sizes),
        compiler_params=pltpu.CompilerParams(collective_id=0, has_side_effects=True),
        name="step",
    )(*values)
    grads = ((weight_first.shape, F32), (weight_second.shape, F32), (weight_third.shape[::-1], F32))
    out = pl.pallas_call(
        functools.partial(finish_kernel, plan, early_sizes, late_sizes),
        out_shape=tuple(jax.ShapeDtypeStruct(*g) for g in grads) + (block,) * 4,
        in_specs=[vmem] * 6, out_specs=(anywhere,) * 7,
        scratch_shapes=[pltpu.VMEM(*g) for g in grads] + [dma((7,))],
        name="finish",
    )(*done)
    return (out[0], out[1], out[2].T) + tuple(v[None, None] for v in out[3:])


def solution(mesh):
    wide, flat, copied = P("row", "col", None, None), P("row", "col", None), P()
    return jax.shard_map(
        functools.partial(per_device, mesh), mesh=mesh,
        in_specs=(wide, wide, wide, flat, flat, wide, wide, wide, wide, wide, copied, copied, copied),
        out_specs=(copied, copied, copied, wide, wide, wide, wide),
        check_vma=False,
    )
```

time: 53.5 us -> 44.9 us (0.84)
  Pallas kernels: 52.5 us -> 43.9 us
    pallas_call x2, Pallas kernels: 52.5 us -> 43.9 us  [the longest x1 41.3 us: per_device(): pl.pallas_call(functools.partial(step_kernel, plan, tiles, early_sizes, l...]
where the time goes in v1:
time: 44.9 us; the launch traced here: 44.7 us
  Pallas kernels  43.9 us (98%)
  between operations  0.81 us (2%)
    pallas_call x1, Pallas kernels, per_device(): pl.pallas_call(functools.partial(step_kernel, plan, tiles, early_sizes, l...  41.3 us
    pallas_call x1, Pallas kernels, per_device(): pl.pallas_call(functools.partial(finish_kernel, plan, early_sizes, late_s...  2.66 us

profile of v1, /device:TPU:0, one launch (start us, length us, event | category | flops | bytes accessed | tf_op | source)
XLA Modules:
  0.0 44.7 jit_solution(4243563556880402571)
XLA Ops:
  0.6 41.3 %step.1 = (bf16[2,16,24,128]{3,2,1,0:T(8,128)(2,1)}, bf16[2,16,40,128]{3,2,1,0:T(8,128)(2,1)}, bf16[512,256]{1,0:T(8,128)(2,1)}, bf16[512,256]{1,0:T(8,128)(2,1)...) custom-call(s32[1024,1024]{1,0:T(8,128)} %bitcast.20, s32[1024,512]{1,0:T(8,128)} %bitcast.21, ...), custom_call_target="tpu_custom_call" | custom-call | tf_op jit(solution)/shard_map/step/pallas_call | solution.py:381
  41.9 2.7 %finish.1 = (f32[602,256]{1,0:T(8,128)}, f32[256,256]{1,0:T(8,128)}, f32[41,256]{1,0:T(8,128)}, bf16[512,256]{1,0:T(8,128)(2,1)}, bf16[512,256]{1,0:T(8,128)(2,1...) custom-call(bf16[2,16,24,128]{3,2,1,0:T(8,128)(2,1)} %get-tuple-element.20.whole_early, ...), custom_call_target="tpu_custom_call" | custom-call | tf_op jit(solution)/shard_map/finish/pallas_call | solution.py:400

commit v2 on v1

--- a/solution.py
+++ b/solution.py
@@ -20,8 +20,7 @@
     return lax.dot_general(a, b, (dims, ((), ())), preferred_element_type=F32)
 
 
-def slope(pre):
-    sigma = jax.nn.sigmoid(pre)
+def slope(pre, sigma):
     return sigma * (1.0 + pre * (1.0 - sigma))
 
 
@@ -98,9 +97,14 @@
         def _():
             copy.start()
 
-        @pl.when(jnp.logical_not(there))
+
+def halo_clear(plan, dsts):
+    bound = dsts[0].shape[0] // 4
+    for k in range(4):
+        @pl.when(jnp.logical_not(plan.edges()[k][2]))
         def _():
-            dst[pl.ds(k * bound, bound), :] = jnp.zeros((bound, dst.shape[1]), dst.dtype)
+            for dst in dsts:
+                dst[pl.ds(k * bound, bound), :] = jnp.zeros((bound, dst.shape[1]), dst.dtype)
 
 
 def halo_finish(plan, src, dst, send, recv, way):
@@ -131,14 +135,16 @@
         self.own[...] = jnp.zeros_like(self.own)
         self.mine[...] = jnp.zeros_like(self.mine)
 
-    def put(self, i, value):
+    def put(self, i, value, row=0):
         at, chunk = slabs(self.sizes, self.plan.chips)[i]
-        for core in range(self.plan.pair):
-            part = value[:, core * self.plan.lanes:(core + 1) * self.plan.lanes]
-            for k in range(-(-value.shape[0] // chunk)):
-                rows = part[k * chunk:(k + 1) * chunk]
-                self.own[core, k, at:at + rows.shape[0], :] = rows
-                self.mine[core, k, at:at + rows.shape[0], :] = rows.astype(BF)
+        end = min(row + value.shape[0], self.sizes[i])
+        for k in range(row // chunk, -(-end // chunk)):
+            low, high = max(row, k * chunk), min(end, (k + 1) * chunk)
+            for core in range(self.plan.pair):
+                part = value[low - row:high - row, core * self.plan.lanes:(core + 1) * self.plan.lanes]
+                place = slice(at + low - k * chunk, at + high - k * chunk)
+                self.own[core, k, place, :] = part
+                self.mine[core, k, place, :] = part.astype(BF)
 
     def pair_copy(self):
         return self.copy(self.mine.at[1 - self.plan.core], self.got_pair, 0, 0, (self.plan.mate, self.plan.c))
@@ -225,114 +231,267 @@
 
 
 SUMMER_REFS = 13
+UNITS, SIDE = 2, 256
 
 
 NAMES = ("local", "halo", "features", "halo_first", "halo_second", "halo_third", "return_second", "return_third",
          "weight_first", "weight_second", "weight_third", "index_row", "labels")
+
+
+def product(accs, lhs, rhs, depth, transpose=False):
+    for k in depth:
+        for q in range(UNITS):
+            pltpu.matmul_push_rhs(rhs(k), staging_register=0, mxu_index=q, transpose=transpose)
+            for i, acc in enumerate(accs[q]):
+                pltpu.matmul_acc_lhs(acc, lhs(q, i, k), load_staged_rhs=0 if i == 0 else None)
+
+
+def padded(value, rows, lanes=None):
+    if value.shape[0] < rows:
+        value = jnp.concatenate([value, jnp.zeros((rows - value.shape[0], value.shape[1]), value.dtype)], axis=0)
+    if lanes is not None and value.shape[1] < lanes:
+        value = jnp.concatenate([value, jnp.zeros((value.shape[0], lanes - value.shape[1]), value.dtype)], axis=1)
+    return value
+
+
+def span(k):
+    return slice(k * SIDE, (k + 1) * SIDE)
 
 
 def step_kernel(plan, tiles, early_sizes, late_sizes, *refs):
     count = len(NAMES)
     hbm = dict(zip(NAMES, refs[:count]))
     whole_early, whole_late, n2, n3, b2, b3 = refs[count:count + 6]
-    held = dict(zip(NAMES, refs[count + 6:2 * count + 6]))
-    (in_sem, local_bf, halo_bf, inverse, hits, hits_t, mixed_one, mixed_two, mixed_three, pre_one, pre_two, hidden_one,
-     hidden_two, scaled, upstream, upstream_three, target_held, s2, s3, o2, o3, hsend, hrecv) = refs[2 * count + 6:2 * count + 29]
-    rest = refs[2 * count + 29:]
+    (in_sem, local_i, halo_i, x_t, values_two, values_three, scaled_three, scaled_two, w1, w2, w3, index_row, labels,
+     near_far, back, halo_t, hits_t, inverse, mixed_t, mixed_two, mixed_two_t, mixed_three, slope_one, slope_two, upstream,
+     upstream_three_t, target_held, w3_wide, s2, s3, o2, o3, hsend, hrecv) = refs[count + 6:count + 40]
+    rest = refs[count + 40:]
     early, late = (Summer(plan, sizes, *part[:5], whole, part[5:]) for sizes, part, whole in (
         (early_sizes, rest[:SUMMER_REFS], whole_early), (late_sizes, rest[SUMMER_REFS:], whole_late)))
-    nodes = held["local"].shape[0]
+    nodes, slots = local_i.shape[0], halo_i.shape[1]
+    every, width, classes = nodes + slots, x_t.shape[0], w3.shape[0]
+    plan.place()
+
+    own, other = pl.ds(0, nodes), pl.ds(nodes, slots)
     tall = nodes // tiles
-    tile = [pl.ds(t * tall, tall) for t in range(tiles)]
-    plan.place()
-
+    tile = [slice(t * tall, (t + 1) * tall) for t in range(tiles)]
+    targets = {"features": x_t.at[:, own], "halo_first": x_t.at[:, other], "halo_second": values_two.at[other],
+               "halo_third": values_three.at[other], "return_second": scaled_two.at[other],
+               "return_third": scaled_three.at[other], "weight_first": w1, "weight_second": w2, "weight_third": w3,
+               "index_row": index_row, "labels": labels}
     loads = {}
-    for name in ("index_row", "features", "halo_first", "local", "halo") + NAMES[4:11] + ("labels",):
-        if name in ("local", "halo"):
-            for t in range(tiles):
-                key = (name, t)
-                loads[key] = pltpu.make_async_copy(hbm[name].at[tile[t]], held[name].at[tile[t]], in_sem.at[len(loads)])
-        else:
-            loads[name] = pltpu.make_async_copy(hbm[name], held[name], in_sem.at[len(loads)])
-    order = ["index_row", "features", "halo_first"]
+
+    def load(key, src, dst):
+        loads[key] = pltpu.make_async_copy(src, dst, in_sem.at[len(loads)])
+        loads[key].start()
+
+    for name in ("index_row", "labels", "features", "halo_first"):
+        load(name, hbm[name], targets[name])
     for t in range(tiles):
-        order += [("local", t), ("halo", t)]
-    order += [name for name in loads if name not in order]
-    for key in order:
-        loads[key].start()
-
+        rows = pl.ds(t * tall, tall)
+        load(("local", t), hbm["local"].at[rows], local_i.at[rows])
+        load(("halo", t), hbm["halo"].at[rows], halo_i.at[rows])
+        if t == 0:
+            load("weight_first", hbm["weight_first"], w1)
+    late_names = NAMES[4:8] + NAMES[9:11]
+    for name in late_names:
+        load(name, hbm[name], targets[name])
+
+    halo_clear(plan, (n2, n3, b2, b3))
     plan.greet()
     early.clear()
     late.clear()
-
     loads["index_row"].wait()
-    slots = hits.shape[1]
-    hits[...] = jnp.where(lax.broadcasted_iota(jnp.int32, (nodes, slots), 0) == held["index_row"][...], 1.0, 0.0).astype(BF)
-    hits_t[...] = hits[...].T
+    back[:, other] = jnp.where(lax.broadcasted_iota(jnp.int32, (nodes, slots), 0) == index_row[...], 1.0, 0.0).astype(BF)
+    hits_t[...] = back[:, other].T
     loads["labels"].wait()
     wide = target_held.shape[1]
-    target_held[...] = jnp.where(lax.broadcasted_iota(jnp.int32, (wide, nodes), 0) == held["labels"][...], 1.0, 0.0).T
-    loads["features"].wait()
-    loads["halo_first"].wait()
-
-    def spread(t, values, remote, out, dims=((1,), (0,))):
-        total = dot(local_bf[tile[t], :], values[...], dims) + dot(halo_bf[tile[t], :], remote[...], dims)
-        out[tile[t], :] = (total * inverse[tile[t], :]).astype(BF)
-
-    for t in range(tiles):
-        loads[("local", t)].wait()
-        loads[("halo", t)].wait()
-        near, far = held["local"][tile[t], :].astype(F32), held["halo"][tile[t], :].astype(F32)
-        here = lax.broadcasted_iota(jnp.int32, near.shape, 0) + t * tall == lax.broadcasted_iota(jnp.int32, near.shape, 1)
-        local_bf[tile[t], :] = jnp.where(here, near + 1.0, near).astype(BF)
-        halo_bf[tile[t], :] = far.astype(BF)
-        inverse[tile[t], :] = 1.0 / (1.0 + jnp.sum(near, axis=1, keepdims=True) + jnp.sum(far, axis=1, keepdims=True))
-        spread(t, held["features"], held["halo_first"], mixed_one, ((1,), (1,)))
-        if t == 0:
-            for name in NAMES[4:11]:
-                loads[name].wait()
-        pre = dot(mixed_one[tile[t], :], held["weight_first"][...])
-        pre_one[tile[t], :] = pre
-        hidden_one[tile[t], :] = (pre * jax.nn.sigmoid(pre)).astype(BF)
-    s2[...] = dot(hits_t[...], hidden_one[...]).astype(BF)
-    halo_start(plan, s2, n2, hsend, hrecv, 0)
-    for t in range(tiles):
-        spread(t, hidden_one, held["halo_second"], mixed_two)
-        pre = dot(mixed_two[tile[t], :], held["weight_second"][...])
-        pre_two[tile[t], :] = pre
-        hidden_two[tile[t], :] = (pre * jax.nn.sigmoid(pre)).astype(BF)
-    s3[...] = dot(hits_t[...], hidden_two[...]).astype(BF)
-    halo_start(plan, s3, n3, hsend, hrecv, 1)
-    for t in range(tiles):
-        spread(t, hidden_two, held["halo_third"], mixed_three)
-        logits = dot(mixed_three[tile[t], :], held["weight_third"][...], ((1,), (1,)))
-        expo = jnp.exp(logits)
-        probs = expo / jnp.sum(expo, axis=1, keepdims=True)
-        target = target_held[tile[t], :logits.shape[1]]
-        up = ((probs - target) / nodes).astype(BF)
-        upstream_three[tile[t], :] = up
-        scaled[tile[t], :] = (dot(up, held["weight_third"][...]) * inverse[tile[t], :]).astype(BF)
-    turn = ((0,), (0,))
-
-    def carry(t, returned):
-        return dot(local_bf[:, tile[t]], scaled[...], turn) + dot(hits[tile[t], :], returned[...])
-
-    for t in range(tiles):
-        upstream[tile[t], :] = (carry(t, held["return_third"]) * slope(pre_two[tile[t], :])).astype(BF)
-    early.put(0, dot(mixed_two[...], upstream[...], turn))
-    early.put(1, dot(upstream_three[...], mixed_three[...], turn))
-    early.start_pair()
-    o3[...] = dot(halo_bf[...], scaled[...], turn).astype(BF)
-    halo_start(plan, o3, b3, hsend, hrecv, 2)
-    for t in range(tiles):
-        across = dot(upstream[tile[t], :], held["weight_second"][...], ((1,), (1,)))
-        scaled[tile[t], :] = (across * inverse[tile[t], :]).astype(BF)
-    early.start_spread()
-    for t in range(tiles):
-        upstream[tile[t], :] = (carry(t, held["return_second"]) * slope(pre_one[tile[t], :])).astype(BF)
-    late.put(0, dot(mixed_one[...], upstream[...], turn))
-    late.start_pair()
-    o2[...] = dot(halo_bf[...], scaled[...], turn).astype(BF)
+    target_held[...] = jnp.where(lax.broadcasted_iota(jnp.int32, (wide, nodes), 0) == labels[...], 1.0, 0.0).T
+    w3_wide[...] = jnp.zeros_like(w3_wide)
+
+    tail = up_to(width, 16 * UNITS) - UNITS * SIDE * (width // (UNITS * SIDE))
+    body = width // (UNITS * SIDE)
+    strip = tail // UNITS
+
+    def first_rows(q, i):
+        return ((q + UNITS * i) * SIDE, SIDE) if i < body else (UNITS * SIDE * body + q * strip, strip)
+
+    def first_layer(*accs):
+        mix = [[accs[q + UNITS * (i + (body + 1) * b)] for q in range(UNITS) for i in range(body + 1)] for b in range(2)]
+        mix = [[m[q * (body + 1):(q + 1) * (body + 1)] for q in range(UNITS)] for m in mix]
+        pres = accs[2 * UNITS * (body + 1):]
+        for acc in accs:
+            pltpu.matmul_pop(acc)
+
+        def gather(t):
+            loads[("local", t)].wait()
+            loads[("halo", t)].wait()
+            near, far = local_i[tile[t], :].astype(F32), halo_i[tile[t], :].astype(F32)
+            total = 1.0 + jnp.sum(near, axis=1, keepdims=True) + jnp.sum(far, axis=1, keepdims=True)
+            near_far[tile[t], own] = near.astype(BF)
+            near_far[tile[t], other] = far.astype(BF)
+            square = near[:, tile[t]]
+            here = lax.broadcasted_iota(jnp.int32, square.shape, 0) == lax.broadcasted_iota(jnp.int32, square.shape, 1)
+            near_far[tile[t], tile[t]] = jnp.where(here, square + 1.0, square).astype(BF)
+            inverse[tile[t], :] = jnp.broadcast_to(1.0 / total, (tall, inverse.shape[1]))
+            if t == 0:
+                loads["features"].wait()
+                loads["halo_first"].wait()
+            product(mix[t % 2], lambda q, i, k: padded(x_t[slice(first_rows(q, i)[0], min(sum(first_rows(q, i)), width)), span(k)], first_rows(q, i)[1]),
+                    lambda k: near_far[tile[t], span(k)], range(every // SIDE), True)
+
+        def settle(t):
+            across = inverse[tile[t], :128].T[0:1]
+            for i in range(body + 1):
+                for q in range(UNITS):
+                    start, size = first_rows(q, i)
+                    mixed_t[start:start + size, tile[t]] = (pltpu.matmul_pop(mix[t % 2][q][i]) * across).astype(BF)
+            back[own, tile[t]] = near_far[tile[t], own].T
+            halo_t[:, tile[t]] = near_far[tile[t], other].T
+            if t == 0:
+                loads["weight_first"].wait()
+            pre_acc = [pres[UNITS * (t % 2) + q] for q in range(UNITS)]
+            half = tall // UNITS
+            depth = -(-width // SIDE)
+            turned = [mixed_t[k * SIDE:min((k + 1) * SIDE, mixed_t.shape[0]), tile[t]].T for k in range(depth)]
+            product([[acc] for acc in pre_acc], lambda q, i, k: padded(turned[k][q * half:(q + 1) * half], half, SIDE),
+                    lambda k: padded(w1[k * SIDE:min((k + 1) * SIDE, width), :], SIDE), range(depth))
+            for q in range(UNITS):
+                rows = slice(t * tall + q * half, t * tall + (q + 1) * half)
+                pre = pltpu.matmul_pop(pre_acc[q])
+                sigma = jax.nn.sigmoid(pre)
+                values_two[rows, :] = (pre * sigma).astype(BF)
+                slope_one[rows, :] = slope(pre, sigma)
+
+        for t in range(tiles):
+            gather(t)
+            if t > 0:
+                settle(t - 1)
+        settle(tiles - 1)
+
+    def accs_of(sizes):
+        return [pltpu.ACC(q)((size, SIDE), F32) for size in sizes for q in range(UNITS)]
+
+    sizes = ([SIDE] * body + [strip]) * 2 + [tall // UNITS] * 2
+    pl.run_scoped(first_layer, *accs_of(sizes))
+
+    for name in late_names:
+        loads[name].wait()
+    w3_wide[0:classes, :] = w3[...]
+    order = list(range(nodes // SIDE, every // SIDE)) + list(range(nodes // SIDE))
+
+    def rest_of_step(*accs):
+        held = [[accs[q + UNITS * i] for i in range(6)] for q in range(UNITS)]
+        first, second = [p[0:2] for p in held], [p[2:3] for p in held]
+        middle, small, small_late = ([p[i] for p in held] for i in (3, 4, 5))
+
+        def at(q, i):
+            return slice((q + UNITS * i) * SIDE, (q + UNITS * i + 1) * SIDE)
+
+        def tall_product(sets, left, right, depth, transpose=False, pieces=2):
+            for i in range(pieces):
+                product([[sets[q][i]] for q in range(UNITS)], lambda q, _, k: left[at(q, i), span(k)],
+                        lambda k: right(k), depth, transpose)
+
+        def pops(sets, use, pieces=2):
+            for i in range(pieces):
+                for q in range(UNITS):
+                    use(at(q, i), pltpu.matmul_pop(sets[q][i]))
+
+        def keep_mixed(mixed, mixed_turned):
+            def use(rows, value):
+                out = (value * inverse[rows, :]).astype(BF)
+                mixed[rows, :] = out
+                if mixed_turned is not None:
+                    mixed_turned[:, rows] = out.T
+            return use
+
+        def keep(out):
+            def use(rows, value):
+                out[rows, :] = value.astype(BF)
+            return use
+
+        def keep_scaled(out):
+            def use(rows, value):
+                out[rows, :] = (value * inverse[rows, :]).astype(BF)
+            return use
+
+        tall_product(first, near_far, lambda k: values_two[span(k), :], order)
+        tall_product(second, hits_t, lambda k: values_two[span(k), :], range(nodes // SIDE), pieces=1)
+        pops(first, keep_mixed(mixed_two, mixed_two_t))
+        tall_product(first, mixed_two, lambda k: w2[...], range(1))
+        pops(second, keep(s2), pieces=1)
+
+        def activate(rows, pre):
+            sigma = jax.nn.sigmoid(pre)
+            values_three[rows, :] = (pre * sigma).astype(BF)
+            slope_two[rows, :] = slope(pre, sigma)
+
+        pops(first, activate)
+        halo_start(plan, s2, n2, hsend, hrecv, 0)
+        tall_product(first, near_far, lambda k: values_three[span(k), :], order)
+        tall_product(second, hits_t, lambda k: values_three[span(k), :], range(nodes // SIDE), pieces=1)
+        pops(first, keep_mixed(mixed_three, None))
+        tall_product(first, mixed_three, lambda k: w3_wide[...], range(1), True)
+        pops(second, keep(s3), pieces=1)
+        ups = {}
+
+        def soften(rows, logits):
+            logits = logits[:, :wide]
+            inside = lax.broadcasted_iota(jnp.int32, logits.shape, 1) < classes
+            expo = jnp.where(inside, jnp.exp(logits), 0.0)
+            probs = expo / jnp.sum(expo, axis=1, keepdims=True)
+            up = ((probs - target_held[rows, :]) / nodes).astype(BF)
+            upstream_three_t[:, rows] = up.T
+            ups[rows.start] = padded(up, up.shape[0], SIDE)
+
+        pops(first, soften)
+        for i in range(2):
+            product([[first[q][i]] for q in range(UNITS)], lambda q, _, k: ups[at(q, i).start], lambda k: w3_wide[...], range(1))
+        pops(first, keep_scaled(scaled_three))
+        halo_start(plan, s3, n3, hsend, hrecv, 1)
+        tall_product(first, back, lambda k: scaled_three[span(k), :], order)
+        stripes = nodes // SIDE // UNITS
+        for k in range(stripes):
+            for q in range(UNITS):
+                pltpu.matmul_push_rhs(mixed_three[span(q * stripes + k), :], staging_register=0, mxu_index=q)
+                pltpu.matmul_acc_lhs(small[q], upstream_three_t[0:small_rows, span(q * stripes + k)], load_staged_rhs=0)
+        tall_product(second, halo_t, lambda k: scaled_three[span(k), :], range(nodes // SIDE), pieces=1)
+
+        def climb(slopes):
+            def use(rows, value):
+                upstream[rows, :] = (value * slopes[rows, :]).astype(BF)
+            return use
+
+        pops(first, climb(slope_two))
+        tall_product(first, upstream, lambda k: w2[...], range(1), True)
+        early.put(1, pltpu.matmul_pop(small[0]) + pltpu.matmul_pop(small[1]))
+        pops(second, keep(o3), pieces=1)
+        half = mixed_two_t.shape[0] // UNITS
+        for k in range(nodes // SIDE):
+            for q in range(UNITS):
+                pltpu.matmul_push_rhs(upstream[span(k), :], staging_register=0, mxu_index=q)
+                pltpu.matmul_acc_lhs(middle[q], mixed_two_t[q * half:(q + 1) * half, span(k)], load_staged_rhs=0)
+        pops(first, keep_scaled(scaled_two))
+        for q in range(UNITS):
+            early.put(0, pltpu.matmul_pop(middle[q]), q * half)
+        early.start_pair()
+        halo_start(plan, o3, b3, hsend, hrecv, 2)
+        tall_product(first, back, lambda k: scaled_two[span(k), :], order)
+        tall_product(second, halo_t, lambda k: scaled_two[span(k), :], range(nodes // SIDE), pieces=1)
+        early.start_spread()
+        pops(first, climb(slope_one))
+        product([first[q][:body] + [small_late[q]] for q in range(UNITS)],
+                lambda q, i, k: mixed_t[slice(first_rows(q, i)[0], sum(first_rows(q, i))), span(k)],
+                lambda k: upstream[span(k), :], range(nodes // SIDE))
+        pops(second, keep(o2), pieces=1)
+        for i in range(body + 1):
+            for q in range(UNITS):
+                late.put(0, pltpu.matmul_pop((first[q][:body] + [small_late[q]])[i]), first_rows(q, i)[0])
+        late.start_pair()
+
+    small_rows = up_to(classes, 16)
+    pl.run_scoped(rest_of_step, *accs_of([SIDE] * 3 + [mixed_two_t.shape[0] // UNITS, small_rows, strip]))
     late.start_spread()
     early.start_gather()
     halo_start(plan, o2, b2, hsend, hrecv, 3)
@@ -375,25 +534,32 @@
     tiles = 4 if nodes % 512 == 0 else 1
     values = (local_mask, halo_mask, features.T, halo_first.T, halo_second, halo_third, return_second, return_third,
               weight_first, weight_second, weight_third.T, index[None, :], labels[None, :])
+    values = tuple(pltpu.with_memory_space_constraint(v, pltpu.HBM) for v in values)
     vmem, anywhere = pl.BlockSpec(memory_space=pltpu.VMEM), pl.BlockSpec(memory_space=pl.ANY)
     dma = pltpu.SemaphoreType.DMA
     block = jax.ShapeDtypeStruct((slots, hidden), BF)
+    every = nodes + slots
+
+    def held(value):
+        return pltpu.VMEM(value.shape, value.dtype)
+
     done = pl.pallas_call(
         functools.partial(step_kernel, plan, tiles, early_sizes, late_sizes),
         out_shape=tuple(jax.ShapeDtypeStruct((plan.pair, plan.chips, slab_rows(sizes, plan.chips), plan.lanes), BF)
                         for sizes in (early_sizes, late_sizes)) + (block,) * 4,
         in_specs=[anywhere] * len(values), out_specs=(vmem,) * 6,
-        scratch_shapes=[pltpu.VMEM(v.shape, v.dtype) for v in values] + [
-            dma((len(values) + 2 * tiles,)), pltpu.VMEM((nodes, nodes), BF), pltpu.VMEM((nodes, slots), BF), pltpu.VMEM((nodes, 1), F32),
-            pltpu.VMEM((nodes, slots), BF), pltpu.VMEM((slots, nodes), BF),
-            pltpu.VMEM((nodes, width), BF), pltpu.VMEM((nodes, hidden), BF), pltpu.VMEM((nodes, hidden), BF),
-            pltpu.VMEM((nodes, hidden), F32), pltpu.VMEM((nodes, hidden), F32),
-            pltpu.VMEM((nodes, hidden), BF), pltpu.VMEM((nodes, hidden), BF), pltpu.VMEM((nodes, hidden), BF),
-            pltpu.VMEM((nodes, hidden), BF), pltpu.VMEM((nodes, classes), BF),
-            pltpu.VMEM((nodes, up_to(classes, 128)), F32)]
+        scratch_shapes=[
+            dma((len(values) + 2 * tiles,)), held(local_mask), held(halo_mask), pltpu.VMEM((width, every), BF),
+            pltpu.VMEM((every, hidden), BF), pltpu.VMEM((every, hidden), BF), pltpu.VMEM((every, hidden), BF),
+            pltpu.VMEM((every, hidden), BF), held(values[8]), held(values[9]), held(values[10]), held(values[11]), held(values[12]),
+            pltpu.VMEM((nodes, every), BF), pltpu.VMEM((nodes, every), BF), pltpu.VMEM((slots, nodes), BF),
+            pltpu.VMEM((slots, nodes), BF), pltpu.VMEM((nodes, hidden), F32), pltpu.VMEM((up_to(width, 16 * UNITS), nodes), BF),
+            pltpu.VMEM((nodes, hidden), BF), pltpu.VMEM((hidden, nodes), BF), pltpu.VMEM((nodes, hidden), BF), pltpu.VMEM((nodes, hidden), F32),
+            pltpu.VMEM((nodes, hidden), F32), pltpu.VMEM((nodes, hidden), BF), pltpu.VMEM((up_to(classes, 128), nodes), BF),
+            pltpu.VMEM((nodes, up_to(classes, 128)), F32), pltpu.VMEM((SIDE, hidden), BF)]
         + [pltpu.VMEM((slots, hidden), BF)] * 4 + [dma((4, 4)), dma((4, 4))]
         + summer_scratch(plan, early_sizes) + summer_scratch(plan, late_sizes),
-        compiler_params=pltpu.CompilerParams(collective_id=0, has_side_effects=True),
+        compiler_params=pltpu.CompilerParams(collective_id=0, has_side_effects=True, vmem_limit_bytes=40 * 2**20),
         name="step",
     )(*values)
     grads = ((weight_first.shape, F32), (weight_second.shape, F32), (weight_third.shape[::-1], F32))
@@ -402,7 +568,7 @@
         out_shape=tuple(jax.ShapeDtypeStruct(*g) for g in grads) + (block,) * 4,
         in_specs=[vmem] * 6, out_specs=(anywhere,) * 7,
         scratch_shapes=[pltpu.VMEM(*g) for g in grads] + [dma((7,))],
-        name="finish",
+        compiler_params=pltpu.CompilerParams(vmem_limit_bytes=16 * 2**20), name="finish",
     )(*done)
     return (out[0], out[1], out[2].T) + tuple(v[None, None] for v in out[3:])
 

time: 44.9 us -> 37.7 us (0.84)
  Pallas kernels: 43.9 us -> 37 us
    pallas_call x1, Pallas kernels: 41.3 us -> 35.6 us  [per_device(): pl.pallas_call(functools.partial(step_kernel, plan, tiles, early_sizes, l...]
    pallas_call x1, Pallas kernels: 2.66 us -> 1.32 us  [per_device(): pl.pallas_call(functools.partial(finish_kernel, plan, early_sizes, late_s...]
where the time goes in v2:
time: 37.7 us; the launch traced here: 37.6 us
  Pallas kernels  37 us (98%)
  between operations  0.65 us (2%)
    pallas_call x1, Pallas kernels, per_device(): pl.pallas_call(functools.partial(step_kernel, plan, tiles, early_sizes, l...  35.6 us
    pallas_call x1, Pallas kernels, per_device(): pl.pallas_call(functools.partial(finish_kernel, plan, early_sizes, late_s...  1.32 us

profile of v2, /device:TPU:0, one launch (start us, length us, event | category | flops | bytes accessed | tf_op | source)
XLA Modules:
  0.0 37.6 jit_solution(15380411771160293016)
XLA Ops:
  0.6 35.6 %step.1 = (bf16[2,16,24,128]{3,2,1,0:T(8,128)(2,1)S(1)}, bf16[2,16,40,128]{3,2,1,0:T(8,128)(2,1)S(1)}, bf16[512,256]{1,0:T(8,128)(2,1)S(1)}, bf16[512,256]{1,0:T...) custom-call(s32[1024,1024]{1,0:T(8,128)} %bitcast.20, s32[1024,512]{1,0:T(8,128)} %bitcast.21, ...), custom_call_target="tpu_custom_call" | custom-call | tf_op jit(solution)/shard_map/step/pallas_call | solution.py:546
  36.3 1.3 %finish.1 = (f32[602,256]{1,0:T(8,128)}, f32[256,256]{1,0:T(8,128)}, f32[41,256]{1,0:T(8,128)}, bf16[512,256]{1,0:T(8,128)(2,1)}, bf16[512,256]{1,0:T(8,128)(2,1...) custom-call(bf16[2,16,24,128]{3,2,1,0:T(8,128)(2,1)S(1)} %get-tuple-element.20.whole_early, ...), custom_call_target="tpu_custom_call" | custom-call | tf_op jit(solution)/shard_map/finish/pallas_call | solution.py:566

commit v3 on v2

--- a/solution.py
+++ b/solution.py
@@ -65,7 +65,7 @@
                 hello((self.r + step, self.c))
         for _, there in self.far_rows():
             count = count + jnp.where(there, 1, 0)
-        pl.semaphore_wait(barrier, count)
+        return lambda: pl.semaphore_wait(barrier, count)
 
     def far_rows(self):
         if self.pair == 2:
@@ -231,6 +231,7 @@
 
 
 SUMMER_REFS = 13
+LATE_AT = 1
 UNITS, SIDE = 2, 256
 
 
@@ -275,39 +276,65 @@
     own, other = pl.ds(0, nodes), pl.ds(nodes, slots)
     tall = nodes // tiles
     tile = [slice(t * tall, (t + 1) * tall) for t in range(tiles)]
-    targets = {"features": x_t.at[:, own], "halo_first": x_t.at[:, other], "halo_second": values_two.at[other],
-               "halo_third": values_three.at[other], "return_second": scaled_two.at[other],
-               "return_third": scaled_three.at[other], "weight_first": w1, "weight_second": w2, "weight_third": w3,
-               "index_row": index_row, "labels": labels}
+    targets = {"features": (x_t, 1, 0), "halo_first": (x_t, 1, nodes), "halo_second": (values_two, 0, nodes),
+               "halo_third": (values_three, 0, nodes), "return_second": (scaled_two, 0, nodes),
+               "return_third": (scaled_three, 0, nodes), "weight_first": (w1, 0, 0), "weight_second": (w2, 0, 0),
+               "weight_third": (w3, 0, 0), "index_row": (index_row, 0, 0), "labels": (labels, 0, 0)}
+    slot = {}
+
+    class Load:
+        def __init__(self, key):
+            self.key = key
+
+        def copy(self):
+            index = slot.setdefault(self.key, len(slot))
+            if isinstance(self.key, tuple):
+                name, t = self.key
+                rows = pl.ds(t * tall, tall)
+                return pltpu.make_async_copy(hbm[name].at[rows], {"local": local_i, "halo": halo_i}[name].at[rows], in_sem.at[index])
+            ref, axis, start = targets[self.key]
+            part = pl.ds(start, hbm[self.key].shape[axis])
+            return pltpu.make_async_copy(hbm[self.key], ref.at[:, part] if axis else ref.at[part], in_sem.at[index])
+
+        def start(self):
+            self.copy().start()
+
+        def wait(self):
+            self.copy().wait()
+
     loads = {}
 
-    def load(key, src, dst):
-        loads[key] = pltpu.make_async_copy(src, dst, in_sem.at[len(loads)])
+    def load(key):
+        loads[key] = Load(key)
         loads[key].start()
 
-    for name in ("index_row", "labels", "features", "halo_first"):
-        load(name, hbm[name], targets[name])
-    for t in range(tiles):
-        rows = pl.ds(t * tall, tall)
-        load(("local", t), hbm["local"].at[rows], local_i.at[rows])
-        load(("halo", t), hbm["halo"].at[rows], halo_i.at[rows])
-        if t == 0:
-            load("weight_first", hbm["weight_first"], w1)
-    late_names = NAMES[4:8] + NAMES[9:11]
-    for name in late_names:
-        load(name, hbm[name], targets[name])
+    late_names = ("halo_second", "halo_third", "return_third", "return_second", "weight_third")
+
+    def load_tile(t):
+        load(("local", t))
+        load(("halo", t))
+
+    def load_named(names):
+        for name in names:
+            load(name)
+
+    load_tile(0)
+    first_names = ("features", "halo_first", "weight_first", "index_row", "labels", "weight_second")
+    load_named(first_names)
+    for t in range(1, tiles):
+        load_tile(t)
 
     halo_clear(plan, (n2, n3, b2, b3))
-    plan.greet()
+    met = plan.greet()
     early.clear()
     late.clear()
-    loads["index_row"].wait()
-    back[:, other] = jnp.where(lax.broadcasted_iota(jnp.int32, (nodes, slots), 0) == index_row[...], 1.0, 0.0).astype(BF)
-    hits_t[...] = back[:, other].T
-    loads["labels"].wait()
     wide = target_held.shape[1]
-    target_held[...] = jnp.where(lax.broadcasted_iota(jnp.int32, (wide, nodes), 0) == labels[...], 1.0, 0.0).T
-    w3_wide[...] = jnp.zeros_like(w3_wide)
+
+    def mark():
+        back[:, other] = jnp.where(lax.broadcasted_iota(jnp.int32, (nodes, slots), 0) == index_row[...], 1.0, 0.0).astype(BF)
+        hits_t[...] = back[:, other].T
+        target_held[...] = jnp.where(lax.broadcasted_iota(jnp.int32, (wide, nodes), 0) == labels[...], 1.0, 0.0).T
+        w3_wide[...] = jnp.zeros_like(w3_wide)
 
     tail = up_to(width, 16 * UNITS) - UNITS * SIDE * (width // (UNITS * SIDE))
     body = width // (UNITS * SIDE)
@@ -326,6 +353,10 @@
         def gather(t):
             loads[("local", t)].wait()
             loads[("halo", t)].wait()
+            if t == LATE_AT:
+                load_named(late_names)
+            if t == tiles - 1:
+                loads[late_names[0]].wait()
             near, far = local_i[tile[t], :].astype(F32), halo_i[tile[t], :].astype(F32)
             total = 1.0 + jnp.sum(near, axis=1, keepdims=True) + jnp.sum(far, axis=1, keepdims=True)
             near_far[tile[t], own] = near.astype(BF)
@@ -334,13 +365,14 @@
             here = lax.broadcasted_iota(jnp.int32, square.shape, 0) == lax.broadcasted_iota(jnp.int32, square.shape, 1)
             near_far[tile[t], tile[t]] = jnp.where(here, square + 1.0, square).astype(BF)
             inverse[tile[t], :] = jnp.broadcast_to(1.0 / total, (tall, inverse.shape[1]))
-            if t == 0:
-                loads["features"].wait()
-                loads["halo_first"].wait()
+
+        def mix_tile(t):
             product(mix[t % 2], lambda q, i, k: padded(x_t[slice(first_rows(q, i)[0], min(sum(first_rows(q, i)), width)), span(k)], first_rows(q, i)[1]),
                     lambda k: near_far[tile[t], span(k)], range(every // SIDE), True)
 
         def settle(t):
+            pre_acc = [pres[UNITS * (t % 2) + q] for q in range(UNITS)]
+            half = tall // UNITS
             across = inverse[tile[t], :128].T[0:1]
             for i in range(body + 1):
                 for q in range(UNITS):
@@ -348,26 +380,36 @@
                     mixed_t[start:start + size, tile[t]] = (pltpu.matmul_pop(mix[t % 2][q][i]) * across).astype(BF)
             back[own, tile[t]] = near_far[tile[t], own].T
             halo_t[:, tile[t]] = near_far[tile[t], other].T
-            if t == 0:
-                loads["weight_first"].wait()
-            pre_acc = [pres[UNITS * (t % 2) + q] for q in range(UNITS)]
-            half = tall // UNITS
             depth = -(-width // SIDE)
             turned = [mixed_t[k * SIDE:min((k + 1) * SIDE, mixed_t.shape[0]), tile[t]].T for k in range(depth)]
             product([[acc] for acc in pre_acc], lambda q, i, k: padded(turned[k][q * half:(q + 1) * half], half, SIDE),
                     lambda k: padded(w1[k * SIDE:min((k + 1) * SIDE, width), :], SIDE), range(depth))
+
+        def close(t):
+            half = tall // UNITS
             for q in range(UNITS):
                 rows = slice(t * tall + q * half, t * tall + (q + 1) * half)
-                pre = pltpu.matmul_pop(pre_acc[q])
+                pre = pltpu.matmul_pop(pres[UNITS * (t % 2) + q])
                 sigma = jax.nn.sigmoid(pre)
                 values_two[rows, :] = (pre * sigma).astype(BF)
                 slope_one[rows, :] = slope(pre, sigma)
 
         for t in range(tiles):
             gather(t)
+            if t == 0:
+                for name in first_names:
+                    loads[name].wait()
+            mix_tile(t)
+            if t == 0:
+                mark()
+            if t > 1:
+                close(t - 2)
             if t > 0:
                 settle(t - 1)
+        if tiles > 1:
+            close(tiles - 2)
         settle(tiles - 1)
+        close(tiles - 1)
 
     def accs_of(sizes):
         return [pltpu.ACC(q)((size, SIDE), F32) for size in sizes for q in range(UNITS)]
@@ -375,9 +417,6 @@
     sizes = ([SIDE] * body + [strip]) * 2 + [tall // UNITS] * 2
     pl.run_scoped(first_layer, *accs_of(sizes))
 
-    for name in late_names:
-        loads[name].wait()
-    w3_wide[0:classes, :] = w3[...]
     order = list(range(nodes // SIDE, every // SIDE)) + list(range(nodes // SIDE))
 
     def rest_of_step(*accs):
@@ -428,6 +467,10 @@
             slope_two[rows, :] = slope(pre, sigma)
 
         pops(first, activate)
+        for name in late_names[1:]:
+            loads[name].wait()
+        w3_wide[0:classes, :] = w3[...]
+        met()
         halo_start(plan, s2, n2, hsend, hrecv, 0)
         tall_product(first, near_far, lambda k: values_three[span(k), :], order)
         tall_product(second, hits_t, lambda k: values_three[span(k), :], range(nodes // SIDE), pieces=1)
@@ -494,11 +537,11 @@
     pl.run_scoped(rest_of_step, *accs_of([SIDE] * 3 + [mixed_two_t.shape[0] // UNITS, small_rows, strip]))
     late.start_spread()
     early.start_gather()
+    late.start_gather()
     halo_start(plan, o2, b2, hsend, hrecv, 3)
-    late.start_gather()
     early.start_back()
+    early.finish()
     late.start_back()
-    early.finish()
     late.finish()
     for way, (src, dst) in enumerate(((s2, n2), (s3, n3), (o3, b3), (o2, b2))):
         halo_finish(plan, src, dst, hsend, hrecv, way)

time: 37.7 us -> 35.3 us (0.936)
  Pallas kernels: 37 us -> 34.5 us
    pallas_call x1, Pallas kernels: 35.6 us -> 33.2 us  [per_device(): pl.pallas_call(functools.partial(step_kernel, plan, tiles, early_sizes, l...]
where the time goes in v3:
time: 35.3 us; the launch traced here: 35.2 us
  Pallas kernels  34.5 us (98%)
  between operations  0.65 us (2%)
    pallas_call x1, Pallas kernels, per_device(): pl.pallas_call(functools.partial(step_kernel, plan, tiles, early_sizes, l...  33.2 us
    pallas_call x1, Pallas kernels, per_device(): pl.pallas_call(functools.partial(finish_kernel, plan, early_sizes, late_s...  1.32 us

profile of v3, /device:TPU:0, one launch (start us, length us, event | category | flops | bytes accessed | tf_op | source)
XLA Modules:
  0.0 35.2 jit_solution(1514921305706907196)
XLA Ops:
  0.6 33.2 %step.1 = (bf16[2,16,24,128]{3,2,1,0:T(8,128)(2,1)S(1)}, bf16[2,16,40,128]{3,2,1,0:T(8,128)(2,1)S(1)}, bf16[512,256]{1,0:T(8,128)(2,1)S(1)}, bf16[512,256]{1,0:T...) custom-call(s32[1024,1024]{1,0:T(8,128)} %bitcast.20, s32[1024,512]{1,0:T(8,128)} %bitcast.21, ...), custom_call_target="tpu_custom_call" | custom-call | tf_op jit(solution)/shard_map/step/pallas_call | solution.py:589
  33.8 1.3 %finish.1 = (f32[602,256]{1,0:T(8,128)}, f32[256,256]{1,0:T(8,128)}, f32[41,256]{1,0:T(8,128)}, bf16[512,256]{1,0:T(8,128)(2,1)}, bf16[512,256]{1,0:T(8,128)(2,1...) custom-call(bf16[2,16,24,128]{3,2,1,0:T(8,128)(2,1)S(1)} %get-tuple-element.20.whole_early, ...), custom_call_target="tpu_custom_call" | custom-call | tf_op jit(solution)/shard_map/finish/pallas_call | solution.py:609

commit v4 on v3

--- a/solution.py
+++ b/solution.py
@@ -31,9 +31,7 @@
         self.deep = self.n_row // self.pair
         self.chips = self.deep * self.n_col
         self.lanes = hidden // self.pair
-        deep = sorted(range(self.deep), key=lambda d: -min(d, self.deep - d))
-        cols = sorted(range(self.n_col), key=lambda d: -min(d, self.n_col - d))
-        self.ways = [(dz, dc) for dz in deep for dc in cols if dz or dc]
+        self.ways = range(self.chips - 1)
 
     def place(self):
         self.r, self.c = lax.axis_index("row"), lax.axis_index("col")
@@ -41,10 +39,10 @@
         self.mate = self.r + 1 - 2 * self.core
         self.chip = self.z * self.n_col + self.c
 
-    def peer(self, way, sign=1):
-        z = (self.z + sign * way[0] + self.deep) % self.deep
-        c = (self.c + sign * way[1] + self.n_col) % self.n_col
-        return z * self.n_col + c, (z * self.pair + self.core, c)
+    def peer(self, way):
+        index = way + jnp.where(way >= self.chip, 1, 0)
+        z, c = index // self.n_col, index % self.n_col
+        return index, (z * self.pair + self.core, c), self.chip - jnp.where(way < self.chip, 1, 0)
 
     def greet(self):
         barrier = pltpu.get_barrier_semaphore()
@@ -73,6 +71,9 @@
                     (1, jnp.logical_and(self.core == 1, self.r < self.n_row - 1)))
         return ()
 
+    def turns(self):
+        return ((3, 1, 3, 2, 2), (2, 2, 0, 1, 3)) if self.n_col == 4 else ()
+
     def edges(self):
         r, c = self.r, self.c
         return (((r - 1, c), 1, r > 0), ((r + 1, c), 0, r < self.n_row - 1),
@@ -88,14 +89,47 @@
     return copy, slot, there
 
 
-def halo_start(plan, src, dst, send, recv, way):
+def halo_start(plan, src, dst, send, recv, way, relay=None):
     bound = src.shape[0] // 4
     for k in range(4):
         copy, _, there = halo_copy(plan, k, src, dst, send, recv, way)
+        turns = [turn for turn in plan.turns() if relay is not None and turn[0] == k]
+        for _, origin, middle, _, _ in turns:
+            there = jnp.logical_and(there, plan.c != origin)
+
+            @pl.when(plan.c == origin)
+            def _():
+                pltpu.make_async_remote_copy(
+                    src_ref=src.at[pl.ds(k * bound, bound)], dst_ref=relay[0].at[way], send_sem=send.at[way, k],
+                    recv_sem=relay[2].at[way], device_id=(plan.r, middle), device_id_type=MESH).start()
 
         @pl.when(there)
         def _():
             copy.start()
+
+
+def relay_copy(plan, turn, dst, recv, way, relay):
+    bound = dst.shape[0] // 4
+    return pltpu.make_async_remote_copy(
+        src_ref=relay[0].at[way], dst_ref=dst.at[pl.ds(turn[4] * bound, bound)], send_sem=relay[1].at[way],
+        recv_sem=recv.at[way, turn[4]], device_id=(plan.r, turn[3]), device_id_type=MESH)
+
+
+def relay_start(plan, dst, recv, way, relay):
+    for turn in plan.turns():
+        @pl.when(plan.c == turn[2])
+        def _():
+            pltpu.make_async_remote_copy(
+                src_ref=relay[0].at[way], dst_ref=relay[0].at[way], send_sem=relay[1].at[way],
+                recv_sem=relay[2].at[way], device_id=(plan.r, turn[1]), device_id_type=MESH).wait_recv()
+            relay_copy(plan, turn, dst, recv, way, relay).start()
+
+
+def relay_finish(plan, dst, recv, way, relay):
+    for turn in plan.turns():
+        @pl.when(plan.c == turn[2])
+        def _():
+            relay_copy(plan, turn, dst, recv, way, relay).wait_send()
 
 
 def halo_clear(plan, dsts):
@@ -126,9 +160,10 @@
         self.plan, self.sizes, self.own, self.mine, self.got_pair = plan, sizes, own, mine, got_pair
         self.acc, self.got, self.whole, self.sems = acc, got, whole, sems
 
-    def copy(self, src, dst, kind, d, device):
+    def copy(self, src, dst, kind, d, device, there=None):
         return pltpu.make_async_remote_copy(
-            src_ref=src, dst_ref=dst, send_sem=self.sems[2 * kind].at[d], recv_sem=self.sems[2 * kind + 1].at[d],
+            src_ref=src, dst_ref=dst, send_sem=self.sems[2 * kind].at[d],
+            recv_sem=self.sems[2 * kind + 1].at[d if there is None else there],
             device_id=device, device_id_type=MESH)
 
     def clear(self):
@@ -154,8 +189,8 @@
             self.pair_copy().start()
 
     def spread_copy(self, d):
-        index, device = self.plan.peer(self.plan.ways[d])
-        return self.copy(self.acc.at[index], self.got.at[d], 1, d, device)
+        index, device, there = self.plan.peer(d)
+        return self.copy(self.acc.at[index], self.got.at[there], 1, d, device, there)
 
     def start_spread(self):
         if self.plan.pair == 2:
@@ -163,15 +198,16 @@
             self.acc[...] = (self.own[self.plan.core] + self.got_pair[...].astype(F32)).astype(BF)
         else:
             self.acc[...] = self.mine[0]
-        for d in range(len(self.plan.ways)):
+        for d in self.plan.ways:
             self.spread_copy(d).start()
 
     def gather_copy(self, d):
+        _, device, there = self.plan.peer(d)
         part = self.whole.at[self.plan.core, self.plan.chip]
-        return self.copy(part, part, 2, d, self.plan.peer(self.plan.ways[d])[1])
+        return self.copy(part, part, 2, d, device, there)
 
     def back_copy(self, d, core):
-        index = self.plan.chip if d == len(self.plan.ways) else self.plan.peer(self.plan.ways[d], -1)[0]
+        index = self.plan.chip if d == len(self.plan.ways) else self.plan.peer(d)[0]
         part = self.whole.at[core, index]
         return self.copy(part, part, 3, d, (self.plan.mate, self.plan.c))
 
@@ -180,28 +216,29 @@
         total = self.own[plan.core, plan.chip]
         if plan.pair == 2:
             total = total + self.got_pair[plan.chip].astype(F32)
-        for d in range(len(plan.ways)):
-            self.spread_copy(d).wait()
-        for d in range(len(plan.ways)):
+        for d in plan.ways:
+            index, device, _ = plan.peer(d)
+            self.spread_copy(d).wait_send()
+            self.copy(self.acc.at[index], self.got.at[d], 1, d, device).wait_recv()
             total = total + self.got[d].astype(F32)
         self.whole[plan.core, plan.chip] = total.astype(BF)
-        for d in range(len(plan.ways)):
+        for d in plan.ways:
             self.gather_copy(d).start()
         if plan.pair == 2:
             self.back_copy(len(plan.ways), plan.core).start()
 
     def start_back(self):
         plan = self.plan
-        for d in reversed(range(len(plan.ways))):
-            index = plan.peer(plan.ways[d], -1)[0]
+        for d in plan.ways:
+            index, device, _ = plan.peer(d)
             part = self.whole.at[plan.core, index]
-            self.copy(part, part, 2, d, plan.peer(plan.ways[d], -1)[1]).wait_recv()
+            self.copy(part, part, 2, d, device).wait_recv()
             if plan.pair == 2:
                 self.back_copy(d, plan.core).start()
 
     def finish(self):
         plan = self.plan
-        for d in range(len(plan.ways)):
+        for d in plan.ways:
             self.gather_copy(d).wait_send()
         if plan.pair == 2:
             for d in range(len(plan.ways) + 1):
@@ -265,8 +302,8 @@
     whole_early, whole_late, n2, n3, b2, b3 = refs[count:count + 6]
     (in_sem, local_i, halo_i, x_t, values_two, values_three, scaled_three, scaled_two, w1, w2, w3, index_row, labels,
      near_far, back, halo_t, hits_t, inverse, mixed_t, mixed_two, mixed_two_t, mixed_three, slope_one, slope_two, upstream,
-     upstream_three_t, target_held, w3_wide, s2, s3, o2, o3, hsend, hrecv) = refs[count + 6:count + 40]
-    rest = refs[count + 40:]
+     upstream_three_t, target_held, w3_wide, s2, s3, o2, o3, hsend, hrecv, *relay) = refs[count + 6:count + 43]
+    rest = refs[count + 43:]
     early, late = (Summer(plan, sizes, *part[:5], whole, part[5:]) for sizes, part, whole in (
         (early_sizes, rest[:SUMMER_REFS], whole_early), (late_sizes, rest[SUMMER_REFS:], whole_late)))
     nodes, slots = local_i.shape[0], halo_i.shape[1]
@@ -471,7 +508,7 @@
             loads[name].wait()
         w3_wide[0:classes, :] = w3[...]
         met()
-        halo_start(plan, s2, n2, hsend, hrecv, 0)
+        halo_start(plan, s2, n2, hsend, hrecv, 0, relay)
         tall_product(first, near_far, lambda k: values_three[span(k), :], order)
         tall_product(second, hits_t, lambda k: values_three[span(k), :], range(nodes // SIDE), pieces=1)
         pops(first, keep_mixed(mixed_three, None))
@@ -492,7 +529,7 @@
         for i in range(2):
             product([[first[q][i]] for q in range(UNITS)], lambda q, _, k: ups[at(q, i).start], lambda k: w3_wide[...], range(1))
         pops(first, keep_scaled(scaled_three))
-        halo_start(plan, s3, n3, hsend, hrecv, 1)
+        halo_start(plan, s3, n3, hsend, hrecv, 1, relay)
         tall_product(first, back, lambda k: scaled_three[span(k), :], order)
         stripes = nodes // SIDE // UNITS
         for k in range(stripes):
@@ -519,6 +556,7 @@
         for q in range(UNITS):
             early.put(0, pltpu.matmul_pop(middle[q]), q * half)
         early.start_pair()
+        relay_start(plan, n2, hrecv, 0, relay)
         halo_start(plan, o3, b3, hsend, hrecv, 2)
         tall_product(first, back, lambda k: scaled_two[span(k), :], order)
         tall_product(second, halo_t, lambda k: scaled_two[span(k), :], range(nodes // SIDE), pieces=1)
@@ -536,6 +574,7 @@
     small_rows = up_to(classes, 16)
     pl.run_scoped(rest_of_step, *accs_of([SIDE] * 3 + [mixed_two_t.shape[0] // UNITS, small_rows, strip]))
     late.start_spread()
+    relay_start(plan, n3, hrecv, 1, relay)
     early.start_gather()
     late.start_gather()
     halo_start(plan, o2, b2, hsend, hrecv, 3)
@@ -543,6 +582,8 @@
     early.finish()
     late.start_back()
     late.finish()
+    relay_finish(plan, n2, hrecv, 0, relay)
+    relay_finish(plan, n3, hrecv, 1, relay)
     for way, (src, dst) in enumerate(((s2, n2), (s3, n3), (o3, b3), (o2, b2))):
         halo_finish(plan, src, dst, hsend, hrecv, way)
 
@@ -600,7 +641,7 @@
             pltpu.VMEM((nodes, hidden), BF), pltpu.VMEM((hidden, nodes), BF), pltpu.VMEM((nodes, hidden), BF), pltpu.VMEM((nodes, hidden), F32),
             pltpu.VMEM((nodes, hidden), F32), pltpu.VMEM((nodes, hidden), BF), pltpu.VMEM((up_to(classes, 128), nodes), BF),
             pltpu.VMEM((nodes, up_to(classes, 128)), F32), pltpu.VMEM((SIDE, hidden), BF)]
-        + [pltpu.VMEM((slots, hidden), BF)] * 4 + [dma((4, 4)), dma((4, 4))]
+        + [pltpu.VMEM((slots, hidden), BF)] * 4 + [dma((4, 4)), dma((4, 4)), pltpu.VMEM((2, slots // 4, hidden), BF), dma((2,)), dma((2,))]
         + summer_scratch(plan, early_sizes) + summer_scratch(plan, late_sizes),
         compiler_params=pltpu.CompilerParams(collective_id=0, has_side_effects=True, vmem_limit_bytes=40 * 2**20),
         name="step",

time: 35.3 us -> 33.3 us (0.943)
  Pallas kernels: 34.5 us -> 32.5 us
    pallas_call x1, Pallas kernels: 33.2 us -> 31.2 us  [per_device(): pl.pallas_call(functools.partial(step_kernel, plan, tiles, early_sizes, l...]
where the time goes in v4:
time: 33.3 us; the launch traced here: 33.2 us
  Pallas kernels  32.5 us (98%)
  between operations  0.65 us (2%)
    pallas_call x1, Pallas kernels, per_device(): pl.pallas_call(functools.partial(step_kernel, plan, tiles, early_sizes, l...  31.2 us
    pallas_call x1, Pallas kernels, per_device(): pl.pallas_call(functools.partial(finish_kernel, plan, early_sizes, late_s...  1.32 us

profile of v4, /device:TPU:0, one launch (start us, length us, event | category | flops | bytes accessed | tf_op | source)
XLA Modules:
  0.0 33.2 jit_solution(13020723745168301852)
XLA Ops:
  0.6 31.2 %step.1 = (bf16[2,16,24,128]{3,2,1,0:T(8,128)(2,1)S(1)}, bf16[2,16,40,128]{3,2,1,0:T(8,128)(2,1)S(1)}, bf16[512,256]{1,0:T(8,128)(2,1)S(1)}, bf16[512,256]{1,0:T...) custom-call(s32[1024,1024]{1,0:T(8,128)} %bitcast.20, s32[1024,512]{1,0:T(8,128)} %bitcast.21, ...), custom_call_target="tpu_custom_call" | custom-call | tf_op jit(solution)/shard_map/step/pallas_call | solution.py:630
  31.8 1.3 %finish.1 = (f32[602,256]{1,0:T(8,128)}, f32[256,256]{1,0:T(8,128)}, f32[41,256]{1,0:T(8,128)}, bf16[512,256]{1,0:T(8,128)(2,1)}, bf16[512,256]{1,0:T(8,128)(2,1...) custom-call(bf16[2,16,24,128]{3,2,1,0:T(8,128)(2,1)S(1)} %get-tuple-element.20.whole_early, ...), custom_call_target="tpu_custom_call" | custom-call | tf_op jit(solution)/shard_map/finish/pallas_call | solution.py:650

commit v5 on v4

--- a/solution.py
+++ b/solution.py
@@ -495,20 +495,20 @@
         tall_product(first, near_far, lambda k: values_two[span(k), :], order)
         tall_product(second, hits_t, lambda k: values_two[span(k), :], range(nodes // SIDE), pieces=1)
         pops(first, keep_mixed(mixed_two, mixed_two_t))
-        tall_product(first, mixed_two, lambda k: w2[...], range(1))
         pops(second, keep(s2), pieces=1)
-
-        def activate(rows, pre):
-            sigma = jax.nn.sigmoid(pre)
-            values_three[rows, :] = (pre * sigma).astype(BF)
-            slope_two[rows, :] = slope(pre, sigma)
-
-        pops(first, activate)
         for name in late_names[1:]:
             loads[name].wait()
         w3_wide[0:classes, :] = w3[...]
         met()
         halo_start(plan, s2, n2, hsend, hrecv, 0, relay)
+        tall_product(first, mixed_two, lambda k: w2[...], range(1))
+
+        def activate(rows, pre):
+            sigma = jax.nn.sigmoid(pre)
+            values_three[rows, :] = (pre * sigma).astype(BF)
+            slope_two[rows, :] = slope(pre, sigma)
+
+        pops(first, activate)
         tall_product(first, near_far, lambda k: values_three[span(k), :], order)
         tall_product(second, hits_t, lambda k: values_three[span(k), :], range(nodes // SIDE), pieces=1)
         pops(first, keep_mixed(mixed_three, None))

time: 33.3 us -> 33.2 us (level)
  no operation moved by 1% of the time
where the time goes in v5:
time: 33.2 us; the launch traced here: 33 us
  Pallas kernels  32.4 us (98%)
  between operations  0.65 us (2%)
    pallas_call x1, Pallas kernels, per_device(): pl.pallas_call(functools.partial(step_kernel, plan, tiles, early_sizes, l...  31.1 us
    pallas_call x1, Pallas kernels, per_device(): pl.pallas_call(functools.partial(finish_kernel, plan, early_sizes, late_s...  1.32 us

profile of v5, /device:TPU:0, one launch (start us, length us, event | category | flops | bytes accessed | tf_op | source)
XLA Modules:
  0.0 33.0 jit_solution(11405933520820854089)
XLA Ops:
  0.6 31.1 %step.1 = (bf16[2,16,24,128]{3,2,1,0:T(8,128)(2,1)S(1)}, bf16[2,16,40,128]{3,2,1,0:T(8,128)(2,1)S(1)}, bf16[512,256]{1,0:T(8,128)(2,1)S(1)}, bf16[512,256]{1,0:T...) custom-call(s32[1024,1024]{1,0:T(8,128)} %bitcast.20, s32[1024,512]{1,0:T(8,128)} %bitcast.21, ...), custom_call_target="tpu_custom_call" | custom-call | tf_op jit(solution)/shard_map/step/pallas_call | solution.py:630
  31.7 1.3 %finish.1 = (f32[602,256]{1,0:T(8,128)}, f32[256,256]{1,0:T(8,128)}, f32[41,256]{1,0:T(8,128)}, bf16[512,256]{1,0:T(8,128)(2,1)}, bf16[512,256]{1,0:T(8,128)(2,1...) custom-call(bf16[2,16,24,128]{3,2,1,0:T(8,128)(2,1)S(1)} %get-tuple-element.20.whole_early, ...), custom_call_target="tpu_custom_call" | custom-call | tf_op jit(solution)/shard_map/finish/pallas_call | solution.py:650
